TPU v7x, 8 devices: a whole 2x2x1 slice. The times are simulated.
8 devices in a mesh: dp: 2 (over z, y), cp: 4 (over x, core).
Axes of the slice: x: 2, y: 2, z: 1, core: 2. Of those that a mesh axis runs over, the one named last changes fastest.
Arguments:
- x_in: bfloat16 [2, 4096, 1152], P('dp', 'cp'), parts along dimension 0
- positions: int32 [2, 4096], P('dp', 'cp'), parts along dimension 0
- dy_out: bfloat16 [2, 4096, 1152], P('dp', 'cp'), parts along dimension 0
- w_query: bfloat16 [1152, 4, 256], replicated
- w_key: bfloat16 [1152, 1, 256], replicated
- w_value: bfloat16 [1152, 1, 256], replicated
- w_out: bfloat16 [4, 256, 1152], replicated
- w_pre: float32 [1152], replicated
- w_post: float32 [1152], replicated
Outputs:
- output 1: bfloat16 [2, 4096, 1152], P('dp', 'cp'), parts along dimension 0
- output 2: bfloat16 [2, 4096, 1152], P('dp', 'cp'), parts along dimension 0
- output 3: float32 [2304, 4, 256], P('dp'), parts along dimension 0
- output 4: float32 [2304, 1, 256], P('dp'), parts along dimension 0
- output 5: float32 [2304, 1, 256], P('dp'), parts along dimension 0
- output 6: float32 [8, 256, 1152], P('dp'), parts along dimension 0
- output 7: float32 [2304], P('dp'), parts along dimension 0
- output 8: float32 [2304], P('dp'), parts along dimension 0
There are 2 independent parts. A program takes and returns all parts, laid end to end along the dimension named above; an argument that names none is the same for every part.
All inputs are finite; a program needn't handle non-finite values.
Results may differ from a plain program's by a relative error of at most 0.02.
Values are sent between devices in bfloat16 or wider.
A program may use at most 1 GiB of HBM per device.

v0:
```python
import jax
import jax.numpy as jnp
from jax import lax
from jax.sharding import PartitionSpec as P

NORM_EPS = 1e-6
SOFT_CAP = 50.0
QUERY_SCALE = 144.0
ROPE_BASE = 10000.0


def rms_scale(values, gain):
    return values * lax.rsqrt(jnp.mean(values * values, axis=-1, keepdims=True) + NORM_EPS) * (1.0 + gain)


def rope_tables(positions, head_dim):
    half = head_dim // 2
    inv_freq = ROPE_BASE ** (jnp.arange(half, dtype=jnp.float32) * (-2.0 / head_dim))
    angles = positions.astype(jnp.float32)[:, :, None, None] * inv_freq
    return jnp.cos(angles), jnp.sin(angles)


def rotate(values, cosine, sine):
    half = values.shape[-1] // 2
    first = values[..., :half]
    second = values[..., half:]
    return jnp.concatenate([first * cosine - second * sine, second * cosine + first * sine], axis=-1)


def rotate_back(values, cosine, sine):
    half = values.shape[-1] // 2
    first = values[..., :half]
    second = values[..., half:]
    return jnp.concatenate([first * cosine + second * sine, second * cosine - first * sine], axis=-1)


def solution(mesh):
    groups = mesh.shape["cp"]
    send_pairs = [(source, (source + 1) % groups) for source in range(groups)]
    rows_contract = (((0,), (0,)), ((), ()))
    cols_contract = (((1,), (1,)), ((), ()))

    def local_step(x_in, positions, dy_out, w_query, w_key, w_value, w_out, w_pre, w_post):
        batch, piece_len, model_dim = x_in.shape
        heads, head_dim = w_query.shape[1], w_query.shape[2]
        kv_heads = w_key.shape[1]
        group = heads // kv_heads
        tokens = batch * piece_len
        wq_flat = w_query.reshape(model_dim, heads * head_dim)
        wk_flat = w_key.reshape(model_dim, kv_heads * head_dim)
        wv_flat = w_value.reshape(model_dim, kv_heads * head_dim)
        wo_flat = w_out.reshape(heads * head_dim, model_dim)
        x_float = x_in.astype(jnp.float32).reshape(tokens, model_dim)
        normed, pre_vjp = jax.vjp(rms_scale, x_float, w_pre)
        act_flat = normed.astype(jnp.bfloat16)
        query_proj = jnp.dot(act_flat, wq_flat, preferred_element_type=jnp.float32).astype(jnp.bfloat16)
        key_proj = jnp.dot(act_flat, wk_flat, preferred_element_type=jnp.float32).astype(jnp.bfloat16)
        value_proj = jnp.dot(act_flat, wv_flat, preferred_element_type=jnp.float32).astype(jnp.bfloat16).reshape(batch, piece_len, kv_heads, head_dim)
        cosine, sine = rope_tables(positions, head_dim)
        query_rot = (rotate(query_proj.astype(jnp.float32).reshape(batch, piece_len, heads, head_dim), cosine, sine) * QUERY_SCALE ** -0.5).astype(jnp.bfloat16).reshape(batch, piece_len, kv_heads, group, head_dim)
        key_rot = rotate(key_proj.astype(jnp.float32).reshape(batch, piece_len, kv_heads, head_dim), cosine, sine).astype(jnp.bfloat16)

        def block_scores(key_blk, pos_blk):
            scores = jnp.einsum("bqngd,bknd->bnqgk", query_rot, key_blk, preferred_element_type=jnp.float32)
            capped = SOFT_CAP * jnp.tanh(scores / SOFT_CAP)
            allowed = pos_blk[:, None, None, None, :] <= positions[:, None, :, None, None]
            return jnp.where(allowed, capped, -1e30), capped

        def absorb(state, key_blk, value_blk, pos_blk):
            run_max, run_sum, out_sum = state
            masked, capped = block_scores(key_blk, pos_blk)
            new_max = jnp.maximum(run_max, jnp.max(masked, axis=-1))
            rescale = jnp.exp(run_max - new_max)
            weights = jnp.exp(masked - new_max[..., None])
            run_sum = run_sum * rescale + jnp.sum(weights, axis=-1)
            out_sum = out_sum * rescale[..., None] + jnp.einsum("bnqgk,bknd->bnqgd", weights.astype(jnp.bfloat16), value_blk, preferred_element_type=jnp.float32)
            return new_max, run_sum, out_sum

        stat_shape = (batch, kv_heads, piece_len, group)
        state = absorb((jnp.full(stat_shape, -1e30, jnp.float32), jnp.zeros(stat_shape, jnp.float32), jnp.zeros(stat_shape + (head_dim,), jnp.float32)), key_rot, value_proj, positions)

        def forward_body(step, carry):
            state, key_blk, value_blk, pos_blk = carry
            key_blk, value_blk, pos_blk = lax.ppermute((key_blk, value_blk, pos_blk), "cp", send_pairs)
            return absorb(state, key_blk, value_blk, pos_blk), key_blk, value_blk, pos_blk

        state = lax.fori_loop(1, groups, forward_body, (state, key_rot, value_proj, positions))[0]
        run_max, run_sum, out_sum = state
        log_sum = run_max + jnp.log(run_sum)
        attn_float = jnp.transpose(out_sum / run_sum[..., None], (0, 2, 1, 3, 4))
        attn_flat = attn_float.astype(jnp.bfloat16).reshape(tokens, heads * head_dim)
        z_out = jnp.dot(attn_flat, wo_flat, preferred_element_type=jnp.float32).astype(jnp.bfloat16)
        post_normed, post_vjp = jax.vjp(rms_scale, z_out.astype(jnp.float32), w_post)
        y_out = (x_float + post_normed.astype(jnp.bfloat16).astype(jnp.float32)).astype(jnp.bfloat16)

        dy_float = dy_out.astype(jnp.float32).reshape(tokens, model_dim)
        dz_float, dw_post_part = post_vjp(dy_float)
        dz_out = dz_float.astype(jnp.bfloat16)
        dw_out_part = lax.dot_general(attn_flat, dz_out, rows_contract, preferred_element_type=jnp.float32)
        d_attn = lax.dot_general(dz_out, wo_flat, cols_contract, preferred_element_type=jnp.float32).astype(jnp.bfloat16).reshape(batch, piece_len, kv_heads, group, head_dim)
        row_dot = jnp.transpose(jnp.sum(d_attn.astype(jnp.float32) * attn_float, axis=-1), (0, 2, 1, 3))

        def gradient_block(dquery_sum, key_blk, value_blk, pos_blk, dkey_sum, dvalue_sum):
            masked, capped = block_scores(key_blk, pos_blk)
            soft_probs = jnp.exp(masked - log_sum[..., None])
            d_probs = jnp.einsum("bqngd,bknd->bnqgk", d_attn, value_blk, preferred_element_type=jnp.float32)
            dvalue_sum = dvalue_sum + jnp.einsum("bnqgk,bqngd->bknd", soft_probs.astype(jnp.bfloat16), d_attn, preferred_element_type=jnp.float32)
            d_scores = (soft_probs * (d_probs - row_dot[..., None]) * (1.0 - (capped / SOFT_CAP) ** 2)).astype(jnp.bfloat16)
            dquery_sum = dquery_sum + jnp.einsum("bnqgk,bknd->bqngd", d_scores, key_blk, preferred_element_type=jnp.float32)
            dkey_sum = dkey_sum + jnp.einsum("bnqgk,bqngd->bknd", d_scores, query_rot, preferred_element_type=jnp.float32)
            return dquery_sum, dkey_sum, dvalue_sum

        kv_zeros = jnp.zeros((batch, piece_len, kv_heads, head_dim), jnp.float32)
        dquery_sum, dkey_sum, dvalue_sum = gradient_block(jnp.zeros((batch, piece_len, kv_heads, group, head_dim), jnp.float32), key_rot, value_proj, positions, kv_zeros, kv_zeros)

        def backward_body(step, carry):
            dquery_sum, key_blk, value_blk, pos_blk, dkey_sum, dvalue_sum = carry
            key_blk, value_blk, pos_blk, dkey_sum, dvalue_sum = lax.ppermute((key_blk, value_blk, pos_blk, dkey_sum, dvalue_sum), "cp", send_pairs)
            dquery_sum, dkey_sum, dvalue_sum = gradient_block(dquery_sum, key_blk, value_blk, pos_blk, dkey_sum, dvalue_sum)
            return dquery_sum, key_blk, value_blk, pos_blk, dkey_sum, dvalue_sum

        carry = lax.fori_loop(1, groups, backward_body, (dquery_sum, key_rot, value_proj, positions, dkey_sum, dvalue_sum))
        dkey_rot, dvalue_rot = lax.ppermute((carry[4], carry[5]), "cp", send_pairs)
        dquery = (rotate_back(carry[0].reshape(batch, piece_len, heads, head_dim), cosine, sine) * QUERY_SCALE ** -0.5).astype(jnp.bfloat16).reshape(tokens, heads * head_dim)
        dkey = rotate_back(dkey_rot, cosine, sine).astype(jnp.bfloat16).reshape(tokens, kv_heads * head_dim)
        dvalue = dvalue_rot.astype(jnp.bfloat16).reshape(tokens, kv_heads * head_dim)
        dw_query_part = lax.dot_general(act_flat, dquery, rows_contract, preferred_element_type=jnp.float32)
        dw_key_part = lax.dot_general(act_flat, dkey, rows_contract, preferred_element_type=jnp.float32)
        dw_value_part = lax.dot_general(act_flat, dvalue, rows_contract, preferred_element_type=jnp.float32)
        d_act = (lax.dot_general(dquery, wq_flat, cols_contract, preferred_element_type=jnp.float32) + lax.dot_general(dkey, wk_flat, cols_contract, preferred_element_type=jnp.float32) + lax.dot_general(dvalue, wv_flat, cols_contract, preferred_element_type=jnp.float32))
        dx_float, dw_pre_part = pre_vjp(d_act)
        dx_in = (dy_float + dx_float).astype(jnp.bfloat16).reshape(batch, piece_len, model_dim)
        sums = lax.psum((dw_query_part, dw_key_part, dw_value_part, dw_out_part, dw_pre_part, dw_post_part), "cp")
        return (y_out.reshape(batch, piece_len, model_dim), dx_in, sums[0].reshape(model_dim, heads, head_dim), sums[1].reshape(model_dim, kv_heads, head_dim), sums[2].reshape(model_dim, kv_heads, head_dim), sums[3].reshape(heads, head_dim, model_dim), sums[4], sums[5])

    seq_spec = P("dp", "cp", None)
    in_specs = (seq_spec, P("dp", "cp"), seq_spec, P(), P(), P(), P(), P(), P())
    out_specs = (seq_spec, seq_spec, P("dp", None, None), P("dp", None, None), P("dp", None, None), P("dp", None, None), P("dp"), P("dp"))
    return jax.shard_map(local_step, mesh=mesh, in_specs=in_specs, out_specs=out_specs, check_vma=False)
```

profile of v0, /device:TPU:0, one launch (start us, length us, event | category | flops | bytes accessed | tf_op | source)
XLA Modules:
  0.0 661.4 jit_solution(17676684778285172300)
XLA Ops:
  14.1 3.5 convolution_convert_fusion.2
  20.2 2.9 copy.78
  23.1 2.9 copy.79
  26.0 2.9 fusion.97
  34.9 2.7 fusion.127
  37.7 4.8 fusion.51
  44.8 5.6 fusion.49
  54.3 11.5 %add_bitcast_fusion = f32[1,1,1024,4,256]{4,2,3,1,0:T(8,128)} fusion(f32[1024,4]{0,1:T(4,128)S(1)} %get-tuple-element.342, f32[1024,4,1024]{0,2,1:T(8,128)} %copy-done.9, f32[1024,4]{0,1:T(4,128)S(1)} %get-tuple-element.344, pred[1024,1024]{0,1:T(8,128)(4,1)S(1)} %broadcast_compare_fusion.2, bf16[1024,256]{1,0:T(8,128)(2,1)} %convolution_convert_fusion.3), kind=kOutput, calls=%fused_computation.100 | convolution fusion | flops 2169503744 | bytes 22577152 | tf_op jit(solution)/shard_map/bnqgk,bknd->bnqgd/dot_general | solution.py:76
  66.6 4.0 fusion.81
  70.6 95.1 %while.42 = (s32[]{:T(128)}, f32[1,1,1024,4]{2,3,1,0:T(4,128)S(1)}, f32[1,1,1024,4]{2,3,1,0:T(4,128)S(1)}, f32[1,1,1024,4,256]{4,2,3,1,0:T(8,128)}, bf16[1,1024,...) while((s32[]{:T(128)}, f32[1,1,1024,4]{2,3,1,0:T(4,128)S(1)}, ...), condition=%wide.region_6.7_spmd, body=%wide.region_3.6_spmd.sunk | while | flops 4356845568 | bytes 72646872 | solution.py:87
  74.1 6.2 collective-permute-done
  80.9 6.0 fusion.195
  87.0 5.6 fusion.197
  94.3 8.7 %bitcast_add_fusion.8 = f32[1,1,1024,4,256]{4,2,3,1,0:T(8,128)} fusion(f32[1,1,1024,4,256]{4,2,3,1,0:T(8,128)} %get-tuple-element.501, f32[1024,4,1024]{0,2,1:T(8,128)S(1)} %get-tuple-element.474, f32[1024,4]{0,1:T(4,128)S(1)} %bitcast.319, pred[1024,1024]{0,1:T(8,128)(4,1)S(1)} %broadcast_compare_fusion.5, f32[1024,4]{0,1:T(4,128)S(1)} %get-tuple-element.475, ...), kind=kOutput, calls=%fused_computation.7.clone.1 | convolution fusion | flops 2170552320 | bytes 26771456 | tf_op jit(solution)/shard_map/while/body/eval_jaxpr/bnqgk,bknd->bnqgd/dot_general | solution.py:76
  105.4 6.2 collective-permute-done
  112.3 6.0 fusion.195
  118.4 5.6 fusion.197
  125.6 8.7 %bitcast_add_fusion.8 = f32[1,1,1024,4,256]{4,2,3,1,0:T(8,128)} fusion(f32[1,1,1024,4,256]{4,2,3,1,0:T(8,128)} %get-tuple-element.501, f32[1024,4,1024]{0,2,1:T(8,128)S(1)} %get-tuple-element.474, f32[1024,4]{0,1:T(4,128)S(1)} %bitcast.319, pred[1024,1024]{0,1:T(8,128)(4,1)S(1)} %broadcast_compare_fusion.5, f32[1024,4]{0,1:T(4,128)S(1)} %get-tuple-element.475, ...), kind=kOutput, calls=%fused_computation.7.clone.1 | convolution fusion | flops 2170552320 | bytes 26771456 | tf_op jit(solution)/shard_map/while/body/eval_jaxpr/bnqgk,bknd->bnqgd/dot_general | solution.py:76
  136.8 6.2 collective-permute-done
  143.7 6.0 fusion.195
  149.7 5.6 fusion.197
  157.0 8.7 %bitcast_add_fusion.8 = f32[1,1,1024,4,256]{4,2,3,1,0:T(8,128)} fusion(f32[1,1,1024,4,256]{4,2,3,1,0:T(8,128)} %get-tuple-element.501, f32[1024,4,1024]{0,2,1:T(8,128)S(1)} %get-tuple-element.474, f32[1024,4]{0,1:T(4,128)S(1)} %bitcast.319, pred[1024,1024]{0,1:T(8,128)(4,1)S(1)} %broadcast_compare_fusion.5, f32[1024,4]{0,1:T(4,128)S(1)} %get-tuple-element.475, ...), kind=kOutput, calls=%fused_computation.7.clone.1 | convolution fusion | flops 2170552320 | bytes 26771456 | tf_op jit(solution)/shard_map/while/body/eval_jaxpr/bnqgk,bknd->bnqgd/dot_general | solution.py:76
  165.7 5.3 copy.49
  171.1 2.8 fusion.92
  173.9 3.4 fusion.78
  179.7 3.2 fusion.75
  182.9 3.3 convolution_convert_fusion.1
  189.7 6.5 fusion.93
  196.2 14.0 %multiply_convert_fusion.1 = bf16[1024,4,1024]{0,2,1:T(8,128)(2,1)} fusion(f32[1024,4,1024]{0,2,1:T(8,128)} %copy-done.9, bf16[1024,4,256]{0,2,1:T(8,128)(2,1)S(1)} %bitcast.315, f32[1024,4]{0,1:T(4,128)S(1)} %fusion.83, f32[1024,4]{0,1:T(4,128)S(1)} %bitcast.350, pred[1024,1024]{0,1:T(8,128)(4,1)S(1)} %copy-done.18, bf16[1024,256]{1,0:T(8,128)(2,1)S(1)} %copy-done.41), kind=kOutput, calls=%fused_computation.44 | convolution fusion | flops 2189426688 | bytes 28868608 | tf_op jit(solution)/shard_map/bqngd,bknd->bnqgk/dot_general | solution.py:106
  210.3 7.0 %convolution_bitcast_fusion.3 = f32[1,1024,1,256]{1,3,2,0:T(8,128)} fusion(bf16[1024,4,1024]{0,2,1:T(8,128)(2,1)} %multiply_convert_fusion.1, f32[1024,4,128]{2,0,1:T(8,128)S(1)} %copy-done.24, f32[1024,4,128]{2,0,1:T(8,128)S(1)} %copy-done.26), kind=kOutput, calls=%fused_computation.120 | convolution fusion | flops 2150629376 | bytes 13631488 | tf_op jit(solution)/shard_map/bnqgk,bqngd->bknd/dot_general | solution.py:110
  217.3 4.4 convolution_bitcast_fusion.2
  228.1 5.5 copy.56
  233.6 159.7 %while.43 = (s32[]{:T(128)}, f32[1,1024,1,4,256]{4,1,3,2,0:T(8,128)}, bf16[1,1024,1,256]{3,1,2,0:T(8,128)(2,1)}, bf16[1,1024,1,256]{3,1,2,0:T(8,128)(2,1)}, s32[...) while((s32[]{:T(128)}, ...), condition=%wide.region_11.12_spmd, body=%wide.region_10.11_spmd.sunk | while | flops 10802954240 | bytes 124338520 | solution.py:122
  236.6 6.1 collective-permute-done.4
  243.4 8.2 %fusion.208 = f32[1024,4,1024]{2,0,1:T(8,128)} fusion(bf16[1,1024,1,4,256]{4,1,3,2,0:T(8,128)(2,1)S(1)} %get-tuple-element.552, bf16[1,1024,1,256]{3,1,2,0:T(8,128)(2,1)S(1)} %collective-permute-done.3), kind=kOutput, calls=%fused_computation.31.clone.1 | convolution fusion | flops 2147483648 | bytes 19398656 | tf_op jit(solution)/shard_map/while/body/eval_jaxpr/bqngd,bknd->bnqgk/dot_general | solution.py:64
  251.5 11.9 %multiply_convert_fusion.3 = bf16[1024,4,1024]{2,0,1:T(8,128)(2,1)S(1)} fusion(f32[1024,4,1024]{2,0,1:T(8,128)} %fusion.208, f32[1024,4]{0,1:T(4,128)S(1)} %bitcast.348, f32[1024,4]{0,1:T(4,128)S(1)} %bitcast.351, pred[1024,1024]{1,0:T(8,128)(4,1)S(1)} %broadcast_compare_fusion.6, bf16[1,1024,1,4,256]{4,1,3,2,0:T(8,128)(2,1)} %get-tuple-element.554, ...), kind=kOutput, calls=%fused_computation.20.clone.1 | convolution fusion | flops 2189426688 | bytes 28868608 | tf_op jit(solution)/shard_map/while/body/eval_jaxpr/bqngd,bknd->bnqgk/dot_general | solution.py:106
  263.4 6.6 bitcast_add_fusion.9
  271.6 4.7 fusion.209
  276.3 10.8 %fusion.210 = f32[1,1024,1,256]{3,1,2,0:T(8,128)} fusion(f32[1,1024,1,256]{3,1,2,0:T(8,128)} %collective-permute-done.7, bf16[1,1024,1,4,256]{4,1,3,2,0:T(8,128)(2,1)S(1)} %copy-done.22, f32[1024,4,1024]{2,0,1:T(8,128)} %fusion.208, f32[1024,4]{0,1:T(4,128)S(1)} %bitcast.352, pred[1024,1024]{1,0:T(8,128)(4,1)S(1)} %broadcast_compare_fusion.6), kind=kOutput, calls=%fused_computation.36.clone.1 | convolution fusion | flops 2168717312 | bytes 22036480 | tf_op jit(solution)/shard_map/while/body/eval_jaxpr/bnqgk,bqngd->bknd/dot_general | solution.py:107
  289.6 6.2 collective-permute-done.4
  296.4 8.2 %fusion.208 = f32[1024,4,1024]{2,0,1:T(8,128)} fusion(bf16[1,1024,1,4,256]{4,1,3,2,0:T(8,128)(2,1)S(1)} %get-tuple-element.552, bf16[1,1024,1,256]{3,1,2,0:T(8,128)(2,1)S(1)} %collective-permute-done.3), kind=kOutput, calls=%fused_computation.31.clone.1 | convolution fusion | flops 2147483648 | bytes 19398656 | tf_op jit(solution)/shard_map/while/body/eval_jaxpr/bqngd,bknd->bnqgk/dot_general | solution.py:64
  304.6 11.9 %multiply_convert_fusion.3 = bf16[1024,4,1024]{2,0,1:T(8,128)(2,1)S(1)} fusion(f32[1024,4,1024]{2,0,1:T(8,128)} %fusion.208, f32[1024,4]{0,1:T(4,128)S(1)} %bitcast.348, f32[1024,4]{0,1:T(4,128)S(1)} %bitcast.351, pred[1024,1024]{1,0:T(8,128)(4,1)S(1)} %broadcast_compare_fusion.6, bf16[1,1024,1,4,256]{4,1,3,2,0:T(8,128)(2,1)} %get-tuple-element.554, ...), kind=kOutput, calls=%fused_computation.20.clone.1 | convolution fusion | flops 2189426688 | bytes 28868608 | tf_op jit(solution)/shard_map/while/body/eval_jaxpr/bqngd,bknd->bnqgk/dot_general | solution.py:106
  316.5 6.6 bitcast_add_fusion.9
  324.7 4.7 fusion.209
  329.4 10.8 %fusion.210 = f32[1,1024,1,256]{3,1,2,0:T(8,128)} fusion(f32[1,1024,1,256]{3,1,2,0:T(8,128)} %collective-permute-done.7, bf16[1,1024,1,4,256]{4,1,3,2,0:T(8,128)(2,1)S(1)} %copy-done.22, f32[1024,4,1024]{2,0,1:T(8,128)} %fusion.208, f32[1024,4]{0,1:T(4,128)S(1)} %bitcast.352, pred[1024,1024]{1,0:T(8,128)(4,1)S(1)} %broadcast_compare_fusion.6), kind=kOutput, calls=%fused_computation.36.clone.1 | convolution fusion | flops 2168717312 | bytes 22036480 | tf_op jit(solution)/shard_map/while/body/eval_jaxpr/bnqgk,bqngd->bknd/dot_general | solution.py:107
  342.6 6.2 collective-permute-done.4
  349.5 8.2 %fusion.208 = f32[1024,4,1024]{2,0,1:T(8,128)} fusion(bf16[1,1024,1,4,256]{4,1,3,2,0:T(8,128)(2,1)S(1)} %get-tuple-element.552, bf16[1,1024,1,256]{3,1,2,0:T(8,128)(2,1)S(1)} %collective-permute-done.3), kind=kOutput, calls=%fused_computation.31.clone.1 | convolution fusion | flops 2147483648 | bytes 19398656 | tf_op jit(solution)/shard_map/while/body/eval_jaxpr/bqngd,bknd->bnqgk/dot_general | solution.py:64
  357.7 11.9 %multiply_convert_fusion.3 = bf16[1024,4,1024]{2,0,1:T(8,128)(2,1)S(1)} fusion(f32[1024,4,1024]{2,0,1:T(8,128)} %fusion.208, f32[1024,4]{0,1:T(4,128)S(1)} %bitcast.348, f32[1024,4]{0,1:T(4,128)S(1)} %bitcast.351, pred[1024,1024]{1,0:T(8,128)(4,1)S(1)} %broadcast_compare_fusion.6, bf16[1,1024,1,4,256]{4,1,3,2,0:T(8,128)(2,1)} %get-tuple-element.554, ...), kind=kOutput, calls=%fused_computation.20.clone.1 | convolution fusion | flops 2189426688 | bytes 28868608 | tf_op jit(solution)/shard_map/while/body/eval_jaxpr/bqngd,bknd->bnqgk/dot_general | solution.py:106
  369.6 6.6 bitcast_add_fusion.9
  377.7 4.7 fusion.209
  382.4 10.8 %fusion.210 = f32[1,1024,1,256]{3,1,2,0:T(8,128)} fusion(f32[1,1024,1,256]{3,1,2,0:T(8,128)} %collective-permute-done.7, bf16[1,1024,1,4,256]{4,1,3,2,0:T(8,128)(2,1)S(1)} %copy-done.22, f32[1024,4,1024]{2,0,1:T(8,128)} %fusion.208, f32[1024,4]{0,1:T(4,128)S(1)} %bitcast.352, pred[1024,1024]{1,0:T(8,128)(4,1)S(1)} %broadcast_compare_fusion.6), kind=kOutput, calls=%fused_computation.36.clone.1 | convolution fusion | flops 2168717312 | bytes 22036480 | tf_op jit(solution)/shard_map/while/body/eval_jaxpr/bnqgk,bqngd->bknd/dot_general | solution.py:107
  400.4 2.9 multiply_add_fusion
  405.2 4.0 copy.61
  409.2 6.8 %fusion.151 = f32[1152,1024]{0,1:T(8,128)} fusion(bf16[1024,1024]{0,1:T(8,128)(2,1)} %bitcast.329, bf16[1,1024,1152]{2,1,0:T(8,128)(2,1)S(1)} %copy-done.7, f32[1152]{0:T(1024)S(1)} %copy-done.43, f32[1024]{0:T(1024)S(1)} %copy-done.47), kind=kOutput, calls=%fused_computation.193 | convolution fusion | flops 2420637696 | bytes 9183744 | tf_op jit(solution)/shard_map/dot_general | solution.py:127
  416.0 6.5 copy.63
  422.5 7.3 %fusion.158 = f32[1024,1152]{1,0:T(8,128)} fusion(bf16[1024,1024]{0,1:T(8,128)(2,1)} %bitcast.328, bf16[1024,1152]{1,0:T(8,128)(2,1)} %copy-done.20), kind=kOutput, calls=%fused_computation.196 | convolution fusion | flops 2415919104 | bytes 9175040 | tf_op jit(solution)/shard_map/dot_general | solution.py:99
  429.8 3.1 convolution_bitcast_fusion
  437.6 5.3 fusion.157
  444.0 4.9 fusion.69
  448.9 11.9 %all-reduce = (f32[1152]{0:T(1024)}, f32[1152]{0:T(1024)}) all-reduce(f32[1152]{0:T(1024)S(1)} %get-tuple-element.272, f32[1152]{0:T(1024)S(1)} %copy-done.50), channel_id=1, replica_groups=mesh['dp'=2,'cp'=4] {'cp'}, use_global_device_ids=true, to_apply=%region_18.19 | all-reduce | flops 2304 | bytes 18432 | tf_op jit(solution)/shard_map/psum | solution.py:133
  460.8 4.8 fusion.84
  465.6 174.6 %all-reduce.4.cloned.1.call-done = (f32[1152,4,256]{2,1,0:T(4,128)}, f32[1152,1,256]{2,0,1:T(8,128)}, f32[1152,1,256]{2,0,1:T(8,128)}, f32[4,256,1152]{2,1,0:T(8,128)}) async-done(((f32[1152,4,256]{2,1,0:T(4,128)}, f32[1152,1,256]{2,0,1:T(8,128)}, f32[1152,1,256]{2,0,1:T(8,128)}, f32[4,256,1152]{2,1,0:T(8,128)}), (f32[1152,4,256]{2,1,0:T(4,128)}, f32[1152,1,256]{2,0,1:T(8,128)}, f32[1152,1,256]{2,0,1:T(8,128)}, ...) | async-done | bytes 11796496 | tf_op jit(solution)/shard_map/psum | solution.py:133
  640.3 4.7 copy.64
  645.0 4.7 copy.65
  (246 shorter events, 83.6 us)
Async XLA Ops:
  7.2 166.7 %copy-start = (bf16[4,256,1152]{2,1,0:T(8,128)(2,1)S(1)}, bf16[4,256,1152]{2,1,0:T(8,128)(2,1)}, u32[]{:S(2)}) copy-start(bf16[4,256,1152]{2,1,0:T(8,128)(2,1)} %param.19) | copy-start | bytes 7077892
  7.2 633.1 %all-reduce.4.cloned.1.call-start = ((), (), s32[]{:S(2)}) async-start(), calls=%async_computation | async-start | bytes 23592960 | tf_op jit(solution)/shard_map/psum | solution.py:133
  7.2 6.9 %copy-start.4 = (bf16[1,1024,1152]{2,1,0:T(8,128)(2,1)S(1)}, bf16[1,1024,1152]{2,1,0:T(8,128)(2,1)}, u32[]{:S(2)}) copy-start(bf16[1,1024,1152]{2,1,0:T(8,128)(2,1)} %param.13) | copy-start | bytes 7077892
  7.3 23.5 %copy-start.52 = (f32[128]{0:T(128)}, f32[128]{0:T(128)S(1)}, u32[]{:S(2)}) copy-start(f32[128]{0:T(128)S(1)} %multiply_power_fusion) | copy-start | bytes 1540
  8.1 22.7 %copy-start.44 = (f32[1,1024]{1,0:T(1,128)}, f32[1,1024]{1,0:T(1,128)S(1)}, u32[]{:S(2)}) copy-start(f32[1,1024]{1,0:T(1,128)S(1)} %convert_element_type.168) | copy-start | bytes 12292
  11.2 31.3 %copy-start.46 = (f32[1024]{0:T(1024)}, f32[1024]{0:T(1024)S(1)}, u32[]{:S(2)}) copy-start(f32[1024]{0:T(1024)S(1)} %fusion.133) | copy-start | bytes 12292
  11.9 30.6 %copy-start.42 = (f32[1152]{0:T(1024)}, f32[1152]{0:T(1024)S(1)}, u32[]{:S(2)}) copy-start(f32[1152]{0:T(1024)S(1)} %broadcast_add_fusion.1) | copy-start | bytes 13828
  20.2 5.8 copy-start.36
  26.0 7.3 %copy-start.35 = (s32[1,1024]{1,0:T(1,128)S(1)}, s32[1,1024]{1,0:T(1,128)}, u32[]{:S(2)}) copy-start(s32[1,1024]{1,0:T(1,128)} %param.14) | copy-start | bytes 12292
  26.0 8.9 %copy-start.12 = (f32[1,1024,4,128]{3,1,2,0:T(8,128)S(1)}, f32[1,1024,4,128]{3,1,2,0:T(8,128)}, u32[]{:S(2)}) copy-start(f32[1,1024,4,128]{3,1,2,0:T(8,128)} %copy.78) | copy-start | bytes 6291460
  26.0 8.9 %copy-start.13 = (f32[1,1024,4,128]{3,1,2,0:T(8,128)S(1)}, f32[1,1024,4,128]{3,1,2,0:T(8,128)}, u32[]{:S(2)}) copy-start(f32[1,1024,4,128]{3,1,2,0:T(8,128)} %copy.79) | copy-start | bytes 6291460
  30.8 6.8 %copy-start.15 = (f32[1024,128]{1,0:T(8,128)}, f32[1024,128]{1,0:T(8,128)S(1)}, u32[]{:S(2)}) copy-start(f32[1024,128]{1,0:T(8,128)S(1)} %get-tuple-element.345) | copy-start | bytes 1572868
  30.8 6.8 %copy-start.16 = (f32[1024,128]{1,0:T(8,128)}, f32[1024,128]{1,0:T(8,128)S(1)}, u32[]{:S(2)}) copy-start(f32[1024,128]{1,0:T(8,128)S(1)} %get-tuple-element.346) | copy-start | bytes 1572868
  34.0 20.3 %copy-start.17 = (pred[1024,1024]{0,1:T(8,128)(4,1)}, pred[1024,1024]{0,1:T(8,128)(4,1)S(1)}, u32[]{:S(2)}) copy-start(pred[1024,1024]{0,1:T(8,128)(4,1)S(1)} %broadcast_compare_fusion.2) | copy-start | bytes 3145732
  37.6 4.9 copy-start.5
  42.4 7.9 %copy-start.9 = (f32[1024,4,1024]{0,2,1:T(8,128)}, f32[1024,4,1024]{0,2,1:T(8,128)S(1)}, u32[]{:S(2)}) copy-start(f32[1024,4,1024]{0,2,1:T(8,128)S(1)} %get-tuple-element.348) | copy-start | bytes 50331652
  54.3 11.5 %copy-start.40 = (bf16[1024,256]{1,0:T(8,128)(2,1)S(1)}, bf16[1024,256]{1,0:T(8,128)(2,1)}, u32[]{:S(2)}) copy-start(bf16[1024,256]{1,0:T(8,128)(2,1)} %convolution_convert_fusion.3) | copy-start | bytes 1572868
  70.6 10.3 %collective-permute-start.1 = (bf16[1,1024,1,256]{3,1,2,0:T(8,128)(2,1)}, bf16[1,1024,1,256]{3,1,2,0:T(8,128)(2,1)S(1)}, u32[]{:S(2)}, u32[]{:S(2)}) collective-permute-start(bf16[1,1024,1,256]{3,1,2,0:T(8,128)(2,1)} %get-tuple-element.502), channel_id=1, source_target_pairs={{0,1},{1,2},{2,3},{3,0},{4,5},{5,6},{6,7},{7,4}} | collective-permute-start | bytes 1572872 | tf_op jit(solution)/shard_map/while/body/eval_jaxpr/ppermute | solution.py:84
  71.5 8.8 %collective-permute-start = (s32[1,1024]{1,0:T(1,128)S(1)}, s32[1,1024]{1,0:T(1,128)S(1)}, u32[]{:S(2)}, u32[]{:S(2)}) collective-permute-start(s32[1,1024]{1,0:T(1,128)S(1)} %get-tuple-element.504), channel_id=1, source_target_pairs={{0,1},{1,2},{2,3},{3,0},{4,5},{5,6},{6,7},{7,4}} | collective-permute-start | bytes 12296 | tf_op jit(solution)/shard_map/while/body/eval_jaxpr/ppermute | solution.py:84
  74.0 19.4 %collective-permute-start.2 = (bf16[1,1024,1,256]{3,1,2,0:T(8,128)(2,1)}, bf16[1,1024,1,256]{3,1,2,0:T(8,128)(2,1)S(1)}, u32[]{:S(2)}, u32[]{:S(2)}) collective-permute-start(bf16[1,1024,1,256]{3,1,2,0:T(8,128)(2,1)} %get-tuple-element.503), channel_id=1, source_target_pairs={{0,1},{1,2},{2,3},{3,0},{4,5},{5,6},{6,7},{7,4}} | collective-permute-start | bytes 1572872 | tf_op jit(solution)/shard_map/while/body/eval_jaxpr/ppermute | solution.py:84
  103.0 9.3 %collective-permute-start.1 = (bf16[1,1024,1,256]{3,1,2,0:T(8,128)(2,1)}, bf16[1,1024,1,256]{3,1,2,0:T(8,128)(2,1)S(1)}, u32[]{:S(2)}, u32[]{:S(2)}) collective-permute-start(bf16[1,1024,1,256]{3,1,2,0:T(8,128)(2,1)} %get-tuple-element.502), channel_id=1, source_target_pairs={{0,1},{1,2},{2,3},{3,0},{4,5},{5,6},{6,7},{7,4}} | collective-permute-start | bytes 1572872 | tf_op jit(solution)/shard_map/while/body/eval_jaxpr/ppermute | solution.py:84
  103.0 8.6 %collective-permute-start = (s32[1,1024]{1,0:T(1,128)S(1)}, s32[1,1024]{1,0:T(1,128)S(1)}, u32[]{:S(2)}, u32[]{:S(2)}) collective-permute-start(s32[1,1024]{1,0:T(1,128)S(1)} %get-tuple-element.504), channel_id=1, source_target_pairs={{0,1},{1,2},{2,3},{3,0},{4,5},{5,6},{6,7},{7,4}} | collective-permute-start | bytes 12296 | tf_op jit(solution)/shard_map/while/body/eval_jaxpr/ppermute | solution.py:84
  105.4 19.4 %collective-permute-start.2 = (bf16[1,1024,1,256]{3,1,2,0:T(8,128)(2,1)}, bf16[1,1024,1,256]{3,1,2,0:T(8,128)(2,1)S(1)}, u32[]{:S(2)}, u32[]{:S(2)}) collective-permute-start(bf16[1,1024,1,256]{3,1,2,0:T(8,128)(2,1)} %get-tuple-element.503), channel_id=1, source_target_pairs={{0,1},{1,2},{2,3},{3,0},{4,5},{5,6},{6,7},{7,4}} | collective-permute-start | bytes 1572872 | tf_op jit(solution)/shard_map/while/body/eval_jaxpr/ppermute | solution.py:84
  134.3 9.3 %collective-permute-start.1 = (bf16[1,1024,1,256]{3,1,2,0:T(8,128)(2,1)}, bf16[1,1024,1,256]{3,1,2,0:T(8,128)(2,1)S(1)}, u32[]{:S(2)}, u32[]{:S(2)}) collective-permute-start(bf16[1,1024,1,256]{3,1,2,0:T(8,128)(2,1)} %get-tuple-element.502), channel_id=1, source_target_pairs={{0,1},{1,2},{2,3},{3,0},{4,5},{5,6},{6,7},{7,4}} | collective-permute-start | bytes 1572872 | tf_op jit(solution)/shard_map/while/body/eval_jaxpr/ppermute | solution.py:84
  134.3 8.6 %collective-permute-start = (s32[1,1024]{1,0:T(1,128)S(1)}, s32[1,1024]{1,0:T(1,128)S(1)}, u32[]{:S(2)}, u32[]{:S(2)}) collective-permute-start(s32[1,1024]{1,0:T(1,128)S(1)} %get-tuple-element.504), channel_id=1, source_target_pairs={{0,1},{1,2},{2,3},{3,0},{4,5},{5,6},{6,7},{7,4}} | collective-permute-start | bytes 12296 | tf_op jit(solution)/shard_map/while/body/eval_jaxpr/ppermute | solution.py:84
  136.8 19.4 %collective-permute-start.2 = (bf16[1,1024,1,256]{3,1,2,0:T(8,128)(2,1)}, bf16[1,1024,1,256]{3,1,2,0:T(8,128)(2,1)S(1)}, u32[]{:S(2)}, u32[]{:S(2)}) collective-permute-start(bf16[1,1024,1,256]{3,1,2,0:T(8,128)(2,1)} %get-tuple-element.503), channel_id=1, source_target_pairs={{0,1},{1,2},{2,3},{3,0},{4,5},{5,6},{6,7},{7,4}} | collective-permute-start | bytes 1572872 | tf_op jit(solution)/shard_map/while/body/eval_jaxpr/ppermute | solution.py:84
  179.7 7.4 %slice-start = ((s8[16777216]{0:T(1024)(128)(4,1)}), s8[4194304]{0:T(1024)(128)(4,1)S(1)}, s32[]{:S(2)}) async-start(s8[16777216]{0:T(1024)(128)(4,1)} %bitcast.311), calls=%async_computation.1 | async-start | bytes 8388608
  179.7 7.4 %slice-start.1 = ((s8[16777216]{0:T(1024)(128)(4,1)}), s8[4194304]{0:T(1024)(128)(4,1)S(1)}, s32[]{:S(2)}) async-start(s8[16777216]{0:T(1024)(128)(4,1)} %bitcast.311), calls=%async_computation.2 | async-start | bytes 8388608
  182.9 6.6 slice-start.3
  186.2 9.9 %copy-start.10 = (bf16[1024,1024]{0,1:T(8,128)(2,1)}, bf16[1024,1024]{0,1:T(8,128)(2,1)S(1)}, u32[]{:S(2)}) copy-start(bf16[1024,1024]{0,1:T(8,128)(2,1)S(1)} %convolution_convert_fusion.1) | copy-start | bytes 6291460
  189.7 6.5 copy-start.41
  196.2 14.0 %copy-start.24 = (f32[1024,4,128]{2,0,1:T(8,128)S(1)}, f32[1024,4,128]{2,0,1:T(8,128)}, u32[]{:S(2)}) copy-start(f32[1024,4,128]{2,0,1:T(8,128)} %copy-done.23) | copy-start | bytes 6291460
  196.2 14.0 %copy-start.26 = (f32[1024,4,128]{2,0,1:T(8,128)S(1)}, f32[1024,4,128]{2,0,1:T(8,128)}, u32[]{:S(2)}) copy-start(f32[1024,4,128]{2,0,1:T(8,128)} %copy-done.25) | copy-start | bytes 6291460
  210.2 7.0 %copy-start.32 = (bf16[1,1024,1,128]{1,3,2,0:T(8,128)(2,1)S(1)}, bf16[1,1024,1,128]{1,3,2,0:T(8,128)(2,1)}, u32[]{:S(2)}) copy-start(bf16[1,1024,1,128]{1,3,2,0:T(8,128)(2,1)} %copy-done.31) | copy-start | bytes 786436
  210.2 7.0 %copy-start.34 = (bf16[1,1024,1,128]{1,3,2,0:T(8,128)(2,1)S(1)}, bf16[1,1024,1,128]{1,3,2,0:T(8,128)(2,1)}, u32[]{:S(2)}) copy-start(bf16[1,1024,1,128]{1,3,2,0:T(8,128)(2,1)} %copy-done.33) | copy-start | bytes 786436
  210.2 7.0 %copy-start.54 = (bf16[1024,4,1024]{0,2,1:T(8,128)(2,1)S(1)}, bf16[1024,4,1024]{0,2,1:T(8,128)(2,1)}, u32[]{:S(2)}) copy-start(bf16[1024,4,1024]{0,2,1:T(8,128)(2,1)} %multiply_convert_fusion.1) | copy-start | bytes 25165828
  228.1 5.5 copy-start.2
  234.0 9.3 %collective-permute-start.3 = (bf16[1,1024,1,256]{3,1,2,0:T(8,128)(2,1)}, bf16[1,1024,1,256]{3,1,2,0:T(8,128)(2,1)S(1)}, u32[]{:S(2)}, u32[]{:S(2)}) collective-permute-start(bf16[1,1024,1,256]{3,1,2,0:T(8,128)(2,1)} %get-tuple-element.533), channel_id=1, source_target_pairs={{0,1},{1,2},{2,3},{3,0},{4,5},{5,6},{6,7},{7,4}} | collective-permute-start | bytes 1572872 | tf_op jit(solution)/shard_map/while/body/eval_jaxpr/ppermute | solution.py:118
  234.1 8.6 %collective-permute-start.4 = (s32[1,1024]{1,0:T(1,128)S(1)}, s32[1,1024]{1,0:T(1,128)S(1)}, u32[]{:S(2)}, u32[]{:S(2)}) collective-permute-start(s32[1,1024]{1,0:T(1,128)S(1)} %get-tuple-element.535), channel_id=1, source_target_pairs={{0,1},{1,2},{2,3},{3,0},{4,5},{5,6},{6,7},{7,4}} | collective-permute-start | bytes 12296 | tf_op jit(solution)/shard_map/while/body/eval_jaxpr/ppermute | solution.py:118
  236.5 15.1 %collective-permute-start.5 = (bf16[1,1024,1,256]{3,1,2,0:T(8,128)(2,1)}, bf16[1,1024,1,256]{3,1,2,0:T(8,128)(2,1)S(1)}, u32[]{:S(2)}, u32[]{:S(2)}) collective-permute-start(bf16[1,1024,1,256]{3,1,2,0:T(8,128)(2,1)} %get-tuple-element.534), channel_id=1, source_target_pairs={{0,1},{1,2},{2,3},{3,0},{4,5},{5,6},{6,7},{7,4}} | collective-permute-start | bytes 1572872 | tf_op jit(solution)/shard_map/while/body/eval_jaxpr/ppermute | solution.py:118
  236.5 35.1 %collective-permute-start.6 = (f32[1,1024,1,256]{3,1,2,0:T(8,128)}, f32[1,1024,1,256]{3,1,2,0:T(8,128)}, u32[]{:S(2)}, u32[]{:S(2)}) collective-permute-start(f32[1,1024,1,256]{3,1,2,0:T(8,128)} %get-tuple-element.536), channel_id=1, source_target_pairs={{0,1},{1,2},{2,3},{3,0},{4,5},{5,6},{6,7},{7,4}} | collective-permute-start | bytes 3145736 | tf_op jit(solution)/shard_map/while/body/eval_jaxpr/ppermute | solution.py:118
  236.5 39.8 %collective-permute-start.7 = (f32[1,1024,1,256]{3,1,2,0:T(8,128)}, f32[1,1024,1,256]{3,1,2,0:T(8,128)}, u32[]{:S(2)}, u32[]{:S(2)}) collective-permute-start(f32[1,1024,1,256]{3,1,2,0:T(8,128)} %get-tuple-element.537), channel_id=1, source_target_pairs={{0,1},{1,2},{2,3},{3,0},{4,5},{5,6},{6,7},{7,4}} | collective-permute-start | bytes 3145736 | tf_op jit(solution)/shard_map/while/body/eval_jaxpr/ppermute | solution.py:118
  287.1 9.3 %collective-permute-start.3 = (bf16[1,1024,1,256]{3,1,2,0:T(8,128)(2,1)}, bf16[1,1024,1,256]{3,1,2,0:T(8,128)(2,1)S(1)}, u32[]{:S(2)}, u32[]{:S(2)}) collective-permute-start(bf16[1,1024,1,256]{3,1,2,0:T(8,128)(2,1)} %get-tuple-element.533), channel_id=1, source_target_pairs={{0,1},{1,2},{2,3},{3,0},{4,5},{5,6},{6,7},{7,4}} | collective-permute-start | bytes 1572872 | tf_op jit(solution)/shard_map/while/body/eval_jaxpr/ppermute | solution.py:118
  287.1 8.6 %collective-permute-start.4 = (s32[1,1024]{1,0:T(1,128)S(1)}, s32[1,1024]{1,0:T(1,128)S(1)}, u32[]{:S(2)}, u32[]{:S(2)}) collective-permute-start(s32[1,1024]{1,0:T(1,128)S(1)} %get-tuple-element.535), channel_id=1, source_target_pairs={{0,1},{1,2},{2,3},{3,0},{4,5},{5,6},{6,7},{7,4}} | collective-permute-start | bytes 12296 | tf_op jit(solution)/shard_map/while/body/eval_jaxpr/ppermute | solution.py:118
  289.5 15.1 %collective-permute-start.5 = (bf16[1,1024,1,256]{3,1,2,0:T(8,128)(2,1)}, bf16[1,1024,1,256]{3,1,2,0:T(8,128)(2,1)S(1)}, u32[]{:S(2)}, u32[]{:S(2)}) collective-permute-start(bf16[1,1024,1,256]{3,1,2,0:T(8,128)(2,1)} %get-tuple-element.534), channel_id=1, source_target_pairs={{0,1},{1,2},{2,3},{3,0},{4,5},{5,6},{6,7},{7,4}} | collective-permute-start | bytes 1572872 | tf_op jit(solution)/shard_map/while/body/eval_jaxpr/ppermute | solution.py:118
  289.5 35.1 %collective-permute-start.6 = (f32[1,1024,1,256]{3,1,2,0:T(8,128)}, f32[1,1024,1,256]{3,1,2,0:T(8,128)}, u32[]{:S(2)}, u32[]{:S(2)}) collective-permute-start(f32[1,1024,1,256]{3,1,2,0:T(8,128)} %get-tuple-element.536), channel_id=1, source_target_pairs={{0,1},{1,2},{2,3},{3,0},{4,5},{5,6},{6,7},{7,4}} | collective-permute-start | bytes 3145736 | tf_op jit(solution)/shard_map/while/body/eval_jaxpr/ppermute | solution.py:118
  289.6 39.8 %collective-permute-start.7 = (f32[1,1024,1,256]{3,1,2,0:T(8,128)}, f32[1,1024,1,256]{3,1,2,0:T(8,128)}, u32[]{:S(2)}, u32[]{:S(2)}) collective-permute-start(f32[1,1024,1,256]{3,1,2,0:T(8,128)} %get-tuple-element.537), channel_id=1, source_target_pairs={{0,1},{1,2},{2,3},{3,0},{4,5},{5,6},{6,7},{7,4}} | collective-permute-start | bytes 3145736 | tf_op jit(solution)/shard_map/while/body/eval_jaxpr/ppermute | solution.py:118
  340.2 9.3 %collective-permute-start.3 = (bf16[1,1024,1,256]{3,1,2,0:T(8,128)(2,1)}, bf16[1,1024,1,256]{3,1,2,0:T(8,128)(2,1)S(1)}, u32[]{:S(2)}, u32[]{:S(2)}) collective-permute-start(bf16[1,1024,1,256]{3,1,2,0:T(8,128)(2,1)} %get-tuple-element.533), channel_id=1, source_target_pairs={{0,1},{1,2},{2,3},{3,0},{4,5},{5,6},{6,7},{7,4}} | collective-permute-start | bytes 1572872 | tf_op jit(solution)/shard_map/while/body/eval_jaxpr/ppermute | solution.py:118
  340.2 8.6 %collective-permute-start.4 = (s32[1,1024]{1,0:T(1,128)S(1)}, s32[1,1024]{1,0:T(1,128)S(1)}, u32[]{:S(2)}, u32[]{:S(2)}) collective-permute-start(s32[1,1024]{1,0:T(1,128)S(1)} %get-tuple-element.535), channel_id=1, source_target_pairs={{0,1},{1,2},{2,3},{3,0},{4,5},{5,6},{6,7},{7,4}} | collective-permute-start | bytes 12296 | tf_op jit(solution)/shard_map/while/body/eval_jaxpr/ppermute | solution.py:118
  342.6 15.1 %collective-permute-start.5 = (bf16[1,1024,1,256]{3,1,2,0:T(8,128)(2,1)}, bf16[1,1024,1,256]{3,1,2,0:T(8,128)(2,1)S(1)}, u32[]{:S(2)}, u32[]{:S(2)}) collective-permute-start(bf16[1,1024,1,256]{3,1,2,0:T(8,128)(2,1)} %get-tuple-element.534), channel_id=1, source_target_pairs={{0,1},{1,2},{2,3},{3,0},{4,5},{5,6},{6,7},{7,4}} | collective-permute-start | bytes 1572872 | tf_op jit(solution)/shard_map/while/body/eval_jaxpr/ppermute | solution.py:118
  342.6 35.1 %collective-permute-start.6 = (f32[1,1024,1,256]{3,1,2,0:T(8,128)}, f32[1,1024,1,256]{3,1,2,0:T(8,128)}, u32[]{:S(2)}, u32[]{:S(2)}) collective-permute-start(f32[1,1024,1,256]{3,1,2,0:T(8,128)} %get-tuple-element.536), channel_id=1, source_target_pairs={{0,1},{1,2},{2,3},{3,0},{4,5},{5,6},{6,7},{7,4}} | collective-permute-start | bytes 3145736 | tf_op jit(solution)/shard_map/while/body/eval_jaxpr/ppermute | solution.py:118
  342.6 39.8 %collective-permute-start.7 = (f32[1,1024,1,256]{3,1,2,0:T(8,128)}, f32[1,1024,1,256]{3,1,2,0:T(8,128)}, u32[]{:S(2)}, u32[]{:S(2)}) collective-permute-start(f32[1,1024,1,256]{3,1,2,0:T(8,128)} %get-tuple-element.537), channel_id=1, source_target_pairs={{0,1},{1,2},{2,3},{3,0},{4,5},{5,6},{6,7},{7,4}} | collective-permute-start | bytes 3145736 | tf_op jit(solution)/shard_map/while/body/eval_jaxpr/ppermute | solution.py:118
  395.9 37.0 %collective-permute-start.8 = (f32[1,1024,1,256]{1,3,2,0:T(8,128)}, f32[1,1024,1,256]{1,3,2,0:T(8,128)S(1)}, u32[]{:S(2)}, u32[]{:S(2)}) collective-permute-start(f32[1,1024,1,256]{1,3,2,0:T(8,128)} %copy.62), channel_id=1, source_target_pairs={{0,1},{1,2},{2,3},{3,0},{4,5},{5,6},{6,7},{7,4}} | collective-permute-start | bytes 3145736 | tf_op jit(solution)/shard_map/ppermute | solution.py:123
  398.0 31.8 %collective-permute-start.9 = (bf16[1,1024,1,256]{3,1,2,0:T(8,128)(2,1)}, bf16[1,1024,1,256]{3,1,2,0:T(8,128)(2,1)}, u32[]{:S(2)}, u32[]{:S(2)}) collective-permute-start(bf16[1,1024,1,256]{3,1,2,0:T(8,128)(2,1)} %convert.64), channel_id=1, source_target_pairs={{0,1},{1,2},{2,3},{3,0},{4,5},{5,6},{6,7},{7,4}} | collective-permute-start | bytes 1572872 | tf_op jit(solution)/shard_map/ppermute | solution.py:123
  403.3 5.9 copy-start.7
  403.3 5.9 copy-start.43
  403.3 5.9 copy-start.47
  437.6 5.3 copy-start.28
  437.6 5.3 copy-start.30
  437.6 5.3 copy-start.37
  444.0 4.9 copy-start.50
  444.0 16.8 %copy-start.49 = (f32[1024]{0:T(1024)S(1)}, f32[1024]{0:T(1024)}, u32[]{:S(2)}) copy-start(f32[1024]{0:T(1024)} %copy-done.48) | copy-start | bytes 12292
  640.3 9.4 %copy-start.14 = (f32[1152,4,256]{2,1,0:T(4,128)S(1)}, f32[1152,4,256]{2,1,0:T(4,128)}, u32[]{:S(2)}) copy-start(f32[1152,4,256]{2,1,0:T(4,128)} %get-tuple-element.559) | copy-start | bytes 14155780
  645.0 7.1 %slice-start.4 = ((s8[4718592]{0:T(1024)(128)(4,1)}), s8[4194304]{0:T(1024)(128)(4,1)S(1)}, s32[]{:S(2)}) async-start(s8[4718592]{0:T(1024)(128)(4,1)} %bitcast.320), calls=%async_computation.5 | async-start | bytes 8388608
  (26 other events, 92.2 us)
Sparse Core Ops, SparseCore 0:
  437.7 202.5 all-reduce.3
where the time goes:
time: 668 us; the launch traced here: 661 us
  matrix products  264 us (40%)
  waiting for transfers between devices  212 us (32%)
  local copies, waits for them, and re-layouts  73.1 us (11%)
  other arithmetic  66.1 us (10%)
  starting transfers between devices  18.3 us (3%)
  between operations  15 us (2%)
  blocking collectives  11.9 us (2%)
    psum x1, waiting for transfers between devices, local_step(): lax.psum((dw_query_part, dw_key_part, dw_value_part, dw_out_part, dw_pre_...  175 us
    dot_general x4, matrix products, gradient_block(): jnp.einsum('bqngd,bknd->bnqgk', d_attn, value_blk, preferred_element_type...  49.7 us
    dot_general x7, matrix products, block_scores(): jnp.einsum('bqngd,bknd->bnqgk', query_rot, key_blk, preferred_element_typ...  47.4 us
    dot_general x4, matrix products, gradient_block(): jnp.einsum('bnqgk,bqngd->bknd', soft_probs.astype(jnp.bfloat16), d_attn,...  38.8 us
    dot_general x4, matrix products, absorb(): jnp.einsum('bnqgk,bknd->bnqgd', weights.astype(jnp.bfloat16), value_blk,...  37.6 us
    unnamed x131, local copies, waits for them, and re-layouts  28.5 us
    dot_general x4, matrix products, gradient_block(): jnp.einsum('bnqgk,bknd->bqngd', d_scores, key_blk, preferred_element_type...  24.1 us
    reduce_sum x4, other arithmetic, absorb(): run_sum = run_sum * rescale + jnp.sum(weights, axis=-1)  22.3 us
  transfers between devices with their start and end apart: 27, of which 7 were waited for; matrix products, arithmetic and copies ran while one was open for 29% of the time, Pallas kernels for 0%

commit v1 on v0

v1 whole, which is shorter than its diff:
```python
import functools
import jax
import jax.numpy as jnp
from jax import lax
from jax.experimental import pallas as pl
from jax.experimental.pallas import tpu as pltpu
from jax.sharding import PartitionSpec as P

CH=512; H=4; D=256
LOG2E=1.4426950408889634
CAPL=50.0*LOG2E
NT=(((1,),(1,)),((),()))
NN=(((1,),(0,)),((),()))

def fwd_kernel(ids, q_ref, k_ref, v_ref, o_ref, ob_ref, l2_ref, acc, lacc, *, nslot, sub):
    r = ids[pl.program_id(0)]
    acc[...] = jnp.zeros_like(acc)
    lacc[...] = jnp.zeros_like(lacc)
    def tile(j, masked):
        k = k_ref[j]; v = v_ref[j]
        steps = [(h,u) for h in range(H) for u in range(CH//sub)]
        def score(h,u):
            return lax.dot_general(q_ref[u*sub:(u+1)*sub, h*D:(h+1)*D], k, NT, preferred_element_type=jnp.float32)
        def soft(s,h,u):
            e = jnp.exp2(jnp.tanh(s*(1/50.0))*CAPL)
            if masked:
                ri = lax.broadcasted_iota(jnp.int32, (sub,CH), 0)+u*sub
                ci = lax.broadcasted_iota(jnp.int32, (sub,CH), 1)
                e = jnp.where(ci<=ri, e, 0.0)
            lacc[h, u*sub:(u+1)*sub] += e[:, :128]+e[:,128:256]+e[:,256:384]+e[:,384:]
            return e.astype(jnp.bfloat16)
        def pv(e,h,u):
            acc[h, u*sub:(u+1)*sub] += lax.dot_general(e, v, NN, preferred_element_type=jnp.float32)
        n = len(steps)
        s = score(*steps[0]); e = None
        for m in range(n):
            s2 = score(*steps[m+1]) if m+1<n else None
            e2 = soft(s, *steps[m])
            if e is not None: pv(e, *steps[m-1])
            s, e = s2, e2
        pv(e, *steps[n-1])
    def body(j, c):
        g = ids[2+j]
        @pl.when(g<r)
        def _(): tile(j, False)
        @pl.when(g==r)
        def _(): tile(j, True)
        return c
    lax.fori_loop(0, nslot, body, 0)
    for h in range(H):
        la = lacc[h]
        l = jnp.sum(la, axis=1, keepdims=True)
        o = acc[h] / l
        o_ref[:, h*D:(h+1)*D] = o
        ob_ref[:, h*D:(h+1)*D] = o.astype(jnp.bfloat16)
        lrow = jnp.sum(la.T, axis=0, keepdims=True)
        l2_ref[0, h:h+1, :] = jnp.log2(lrow)

def flash_fwd(ids, q, k, v, sub=256):
    n = q.shape[0]//CH; ns = k.shape[0]
    return pl.pallas_call(
        functools.partial(fwd_kernel, nslot=ns, sub=sub),
        grid_spec=pltpu.PrefetchScalarGridSpec(
            num_scalar_prefetch=1, grid=(n,),
            in_specs=[pl.BlockSpec((CH,H*D), lambda i,ids:(i,0)),
                      pl.BlockSpec((ns,CH,D), lambda i,ids:(0,0,0)),
                      pl.BlockSpec((ns,CH,D), lambda i,ids:(0,0,0))],
            out_specs=[pl.BlockSpec((CH,H*D), lambda i,ids:(i,0)),
                       pl.BlockSpec((CH,H*D), lambda i,ids:(i,0)),
                       pl.BlockSpec((1,8,CH), lambda i,ids:(i,0,0))],
            scratch_shapes=[pltpu.VMEM((H,CH,D),jnp.float32), pltpu.VMEM((H,CH,128),jnp.float32)]),
        out_shape=[jax.ShapeDtypeStruct((n*CH,H*D),jnp.float32), jax.ShapeDtypeStruct((n*CH,H*D),jnp.bfloat16),
                   jax.ShapeDtypeStruct((n,8,CH),jnp.float32)],
        compiler_params=pltpu.CompilerParams(dimension_semantics=("arbitrary",), vmem_limit_bytes=60<<20),
        name="flash_fwd",
    )(ids, q, k, v)

def bwd_kernel(ids, q_ref, do_ref, o_ref, l2_ref, k_ref, v_ref, cos_ref, sin_ref, dki_ref, dvi_ref, dq_ref, dk_ref, dv_ref, dqt, pt, dst, dlt, *, nslot, sub):
    i = pl.program_id(0)
    r = ids[i]
    @pl.when(i==0)
    def _():
        dk_ref[...] = dki_ref[...]
        dv_ref[...] = dvi_ref[...]
    dqt[...] = jnp.zeros_like(dqt)
    for h in range(H):
        w = do_ref[:, h*D:(h+1)*D].astype(jnp.float32)*o_ref[:, h*D:(h+1)*D]
        w = w[:, :128]+w[:, 128:]
        dlt[h:h+1, :] = jnp.sum(w.T, axis=0, keepdims=True)
    def tile(j, masked):
        k = k_ref[j]; v = v_ref[j]
        kt = k.T
        steps = [(h,u) for h in range(H) for u in range(CH//sub)]
        def score(h,u):
            cols = slice(u*sub,(u+1)*sub)
            return (lax.dot_general(k, q_ref[cols, h*D:(h+1)*D], NT, preferred_element_type=jnp.float32),
                    lax.dot_general(v, do_ref[cols, h*D:(h+1)*D], NT, preferred_element_type=jnp.float32))
        def soft(sd,h,u):
            s, dp = sd
            cols = slice(u*sub,(u+1)*sub)
            t = jnp.tanh(s*(1/50.0))
            p = jnp.exp2(t*CAPL - l2_ref[0, h:h+1, cols])
            if masked:
                ki = lax.broadcasted_iota(jnp.int32, (CH,sub), 0)
                qi = lax.broadcasted_iota(jnp.int32, (CH,sub), 1)+u*sub
                p = jnp.where(ki<=qi, p, 0.0)
            ds = p*(dp-dlt[h:h+1, cols])*(1.0-t*t)
            dsb = ds.astype(jnp.bfloat16)
            c0 = h*CH+u*sub
            pt[:, c0:c0+sub] = p.astype(jnp.bfloat16)
            dst[:, c0:c0+sub] = dsb
            return dsb
        def dqs(dsb,h,u):
            c0 = h*CH+u*sub
            dqt[:, c0:c0+sub] += lax.dot_general(kt, dsb, NN, preferred_element_type=jnp.float32)
        n = len(steps)
        s = score(*steps[0]); e = None
        for m in range(n):
            s2 = score(*steps[m+1]) if m+1<n else None
            e2 = soft(s, *steps[m])
            if e is not None: dqs(e, *steps[m-1])
            s, e = s2, e2
        dqs(e, *steps[n-1])
        dv_ref[j] += sum(lax.dot_general(pt[:, h*CH:(h+1)*CH], do_ref[:, h*D:(h+1)*D], NN, preferred_element_type=jnp.float32) for h in range(H))
        dk_ref[j] += sum(lax.dot_general(dst[:, h*CH:(h+1)*CH], q_ref[:, h*D:(h+1)*D], NN, preferred_element_type=jnp.float32) for h in range(H))
    def body(j, c):
        g = ids[2+j]
        @pl.when(g<r)
        def _(): tile(j, False)
        @pl.when(g==r)
        def _(): tile(j, True)
        return c
    lax.fori_loop(0, nslot, body, 0)
    c = cos_ref[...]; s = sin_ref[...]
    for h in range(H):
        x = dqt[:, h*CH:(h+1)*CH].T
        a = x[:, :128]; b = x[:, 128:]
        dq_ref[:, h*D:h*D+128] = ((a*c+b*s)*(1/12.0)).astype(jnp.bfloat16)
        dq_ref[:, h*D+128:(h+1)*D] = ((b*c-a*s)*(1/12.0)).astype(jnp.bfloat16)

def flash_bwd(ids, q, do, o, l2, k, v, cos, sin, dki, dvi, sub=256):
    n = q.shape[0]//CH; ns = k.shape[0]
    row = lambda i,ids:(i,0)
    full = lambda i,ids:(0,0,0)
    return pl.pallas_call(
        functools.partial(bwd_kernel, nslot=ns, sub=sub),
        grid_spec=pltpu.PrefetchScalarGridSpec(
            num_scalar_prefetch=1, grid=(n,),
            in_specs=[pl.BlockSpec((CH,H*D), row), pl.BlockSpec((CH,H*D), row), pl.BlockSpec((CH,H*D), row),
                      pl.BlockSpec((1,8,CH), lambda i,ids:(i,0,0)),
                      pl.BlockSpec((ns,CH,D), full, pipeline_mode=pl.Buffered(1)), pl.BlockSpec((ns,CH,D), full, pipeline_mode=pl.Buffered(1)),
                      pl.BlockSpec((CH,128), row), pl.BlockSpec((CH,128), row),
                      pl.BlockSpec((ns,CH,D), full, pipeline_mode=pl.Buffered(1)), pl.BlockSpec((ns,CH,D), full, pipeline_mode=pl.Buffered(1))],
            out_specs=[pl.BlockSpec((CH,H*D), row), pl.BlockSpec((ns,CH,D), full), pl.BlockSpec((ns,CH,D), full)],
            scratch_shapes=[pltpu.VMEM((D,H*CH),jnp.float32), pltpu.VMEM((CH,H*CH),jnp.bfloat16), pltpu.VMEM((CH,H*CH),jnp.bfloat16), pltpu.VMEM((8,CH),jnp.float32)]),
        out_shape=[jax.ShapeDtypeStruct((n*CH,H*D),jnp.bfloat16), jax.ShapeDtypeStruct((ns,CH,D),jnp.float32), jax.ShapeDtypeStruct((ns,CH,D),jnp.float32)],
        compiler_params=pltpu.CompilerParams(dimension_semantics=("arbitrary",), vmem_limit_bytes=63<<20),
        name="flash_bwd",
    )(ids, q, do, o, l2, k, v, cos, sin, dki, dvi)

TN=(((0,),(0,)),((),()))
EPS=1e-6
BR=512

def proj_kernel(x_ref, cos_ref, sin_ref, wp_ref, wq_ref, wk_ref, wv_ref, a_ref, q_ref, k_ref, v_ref):
    x = x_ref[...].astype(jnp.float32)
    rinv = lax.rsqrt(jnp.mean(x*x, axis=-1, keepdims=True)+EPS)
    a = (x*rinv*(1.0+wp_ref[...])).astype(jnp.bfloat16)
    a_ref[...] = a
    c = cos_ref[...]; s = sin_ref[...]
    def rope(y, scale):
        y = y.astype(jnp.bfloat16).astype(jnp.float32)
        f = y[:, :128]; g = y[:, 128:]
        return ((f*c-g*s)*scale).astype(jnp.bfloat16), ((g*c+f*s)*scale).astype(jnp.bfloat16)
    for h in range(H):
        q = lax.dot_general(a, wq_ref[:, h*D:(h+1)*D], NN, preferred_element_type=jnp.float32)
        f, g = rope(q, 1/12.0)
        q_ref[:, h*D:h*D+128] = f
        q_ref[:, h*D+128:(h+1)*D] = g
    f, g = rope(lax.dot_general(a, wk_ref[...], NN, preferred_element_type=jnp.float32), 1.0)
    k_ref[:, :128] = f
    k_ref[:, 128:] = g
    v_ref[...] = lax.dot_general(a, wv_ref[...], NN, preferred_element_type=jnp.float32).astype(jnp.bfloat16)

def proj(x, cos, sin, wp, wq, wk, wv):
    t, m = x.shape
    row = lambda i: (i,0)
    const = lambda i: (0,0)
    one = pl.Buffered(1)
    return pl.pallas_call(
        proj_kernel, grid=(t//BR,),
        in_specs=[pl.BlockSpec((BR,m),row), pl.BlockSpec((BR,128),row), pl.BlockSpec((BR,128),row), pl.BlockSpec((1,m),const),
                  pl.BlockSpec(wq.shape,const,pipeline_mode=one), pl.BlockSpec(wk.shape,const,pipeline_mode=one), pl.BlockSpec(wv.shape,const,pipeline_mode=one)],
        out_specs=[pl.BlockSpec((BR,m),row), pl.BlockSpec((BR,H*D),row), pl.BlockSpec((BR,D),row), pl.BlockSpec((BR,D),row)],
        out_shape=[jax.ShapeDtypeStruct((t,m),jnp.bfloat16), jax.ShapeDtypeStruct((t,H*D),jnp.bfloat16),
                   jax.ShapeDtypeStruct((t,D),jnp.bfloat16), jax.ShapeDtypeStruct((t,D),jnp.bfloat16)],
        compiler_params=pltpu.CompilerParams(dimension_semantics=("arbitrary",), vmem_limit_bytes=60<<20),
        cost_estimate=pl.CostEstimate(flops=2*t*m*1536, bytes_accessed=t*m*8, transcendentals=0),
        name="proj",
    )(x, cos, sin, wp, wq, wk, wv)

def post_kernel(o_ref, x_ref, dy_ref, wp_ref, wo_ref, dwi_ref, y_ref, do_ref, dwo_ref, dwp_ref, *, first):
    i = pl.program_id(0)
    @pl.when(i==0)
    def _():
        dwp_ref[...] = jnp.zeros_like(dwp_ref)
        dwo_ref[...] = jnp.zeros_like(dwo_ref) if first else dwi_ref[...]
    o = o_ref[...]
    z = lax.dot_general(o, wo_ref[...], NN, preferred_element_type=jnp.float32).astype(jnp.bfloat16).astype(jnp.float32)
    rinv = lax.rsqrt(jnp.mean(z*z, axis=-1, keepdims=True)+EPS)
    zh = z*rinv
    gain = 1.0+wp_ref[...]
    y_ref[...] = (x_ref[...].astype(jnp.float32)+(zh*gain).astype(jnp.bfloat16).astype(jnp.float32)).astype(jnp.bfloat16)
    dy = dy_ref[...].astype(jnp.float32)
    dwp_ref[...] += jnp.sum(dy*zh, axis=0, keepdims=True)
    g = dy*gain
    dz = (rinv*(g-zh*jnp.mean(g*zh, axis=-1, keepdims=True))).astype(jnp.bfloat16)
    do_ref[...] = lax.dot_general(dz, wo_ref[...], NT, preferred_element_type=jnp.float32).astype(jnp.bfloat16)
    dwo_ref[...] += lax.dot_general(o, dz, TN, preferred_element_type=jnp.float32)

def post(o, x, dy, wp, wo, dwi):
    t, m = x.shape
    first = dwi is None
    row = lambda i: (i,0)
    const = lambda i: (0,0)
    one = pl.Buffered(1)
    if first:
        dwi = jnp.zeros((8,128), jnp.float32)
    return pl.pallas_call(
        functools.partial(post_kernel, first=first), grid=(t//BR,),
        in_specs=[pl.BlockSpec((BR,H*D),row), pl.BlockSpec((BR,m),row), pl.BlockSpec((BR,m),row), pl.BlockSpec((1,m),const),
                  pl.BlockSpec(wo.shape,const,pipeline_mode=one), pl.BlockSpec(dwi.shape,const,pipeline_mode=one)],
        out_specs=[pl.BlockSpec((BR,m),row), pl.BlockSpec((BR,H*D),row), pl.BlockSpec((H*D,m),const), pl.BlockSpec((1,m),const)],
        out_shape=[jax.ShapeDtypeStruct((t,m),jnp.bfloat16), jax.ShapeDtypeStruct((t,H*D),jnp.bfloat16),
                   jax.ShapeDtypeStruct((H*D,m),jnp.float32), jax.ShapeDtypeStruct((1,m),jnp.float32)],
        compiler_params=pltpu.CompilerParams(dimension_semantics=("arbitrary",), vmem_limit_bytes=60<<20),
        cost_estimate=pl.CostEstimate(flops=6*t*m*1024, bytes_accessed=t*m*8, transcendentals=0),
        name="post",
    )(o, x, dy, wp, wo, dwi)

def last_kernel(a_ref, dq_ref, dk_ref, dv_ref, x_ref, dy_ref, wp_ref, wq_ref, wk_ref, wv_ref, dwq_ref, dwk_ref, dwv_ref, dx_ref, dwp_ref):
    i = pl.program_id(0)
    a = a_ref[...]; dq = dq_ref[...]; dk = dk_ref[...]; dv = dv_ref[...]
    @pl.when(i==0)
    def _():
        dwp_ref[...] = jnp.zeros_like(dwp_ref)
        dwq_ref[...] = jnp.zeros_like(dwq_ref)
        dwk_ref[...] = jnp.zeros_like(dwk_ref)
        dwv_ref[...] = jnp.zeros_like(dwv_ref)
    dwq_ref[...] += lax.dot_general(a, dq, TN, preferred_element_type=jnp.float32)
    dwk_ref[...] += lax.dot_general(a, dk, TN, preferred_element_type=jnp.float32)
    dwv_ref[...] += lax.dot_general(a, dv, TN, preferred_element_type=jnp.float32)
    @pl.when(i<1024//BR)
    def _():
        da = lax.dot_general(dq, wq_ref[...], NT, preferred_element_type=jnp.float32)
        da += lax.dot_general(dk, wk_ref[...], NT, preferred_element_type=jnp.float32)
        da += lax.dot_general(dv, wv_ref[...], NT, preferred_element_type=jnp.float32)
        x = x_ref[...].astype(jnp.float32)
        rinv = lax.rsqrt(jnp.mean(x*x, axis=-1, keepdims=True)+EPS)
        xh = x*rinv
        dwp_ref[...] += jnp.sum(da*xh, axis=0, keepdims=True)
        g = da*(1.0+wp_ref[...])
        dx_ref[...] = (dy_ref[...].astype(jnp.float32)+rinv*(g-xh*jnp.mean(g*xh, axis=-1, keepdims=True))).astype(jnp.bfloat16)

def last(a, dq, dk, dv, x, dy, wp, wq, wk, wv):
    t, m = a.shape
    row = lambda i: (i,0)
    const = lambda i: (0,0)
    half = lambda i: (jnp.minimum(i,1024//BR-1),0)
    one = pl.Buffered(1)
    return pl.pallas_call(
        last_kernel, grid=(t//BR,),
        in_specs=[pl.BlockSpec((BR,m),row), pl.BlockSpec((BR,H*D),row), pl.BlockSpec((BR,D),row), pl.BlockSpec((BR,D),row),
                  pl.BlockSpec((BR,m),half), pl.BlockSpec((BR,m),half), pl.BlockSpec((1,m),const),
                  pl.BlockSpec(wq.shape,const,pipeline_mode=one), pl.BlockSpec(wk.shape,const,pipeline_mode=one), pl.BlockSpec(wv.shape,const,pipeline_mode=one)],
        out_specs=[pl.BlockSpec((m,H*D),const), pl.BlockSpec((m,D),const), pl.BlockSpec((m,D),const), pl.BlockSpec((BR,m),half), pl.BlockSpec((1,m),const)],
        out_shape=[jax.ShapeDtypeStruct((m,H*D),jnp.float32), jax.ShapeDtypeStruct((m,D),jnp.float32), jax.ShapeDtypeStruct((m,D),jnp.float32),
                   jax.ShapeDtypeStruct((1024,m),jnp.bfloat16), jax.ShapeDtypeStruct((1,m),jnp.float32)],
        compiler_params=pltpu.CompilerParams(dimension_semantics=("arbitrary",), vmem_limit_bytes=62<<20),
        cost_estimate=pl.CostEstimate(flops=3*t*m*1536, bytes_accessed=t*m*8, transcendentals=0),
        name="last",
    )(a, dq, dk, dv, x, dy, wp, wq, wk, wv)

ROPE_BASE = 10000.0

def tables(pos):
    inv = ROPE_BASE ** (jnp.arange(128, dtype=jnp.float32)*(-2.0/256))
    ang = pos.astype(jnp.float32)[:, None]*inv
    return jnp.cos(ang), jnp.sin(ang)

def solution(mesh):
    def local_step(x_in, positions, dy_out, w_query, w_key, w_value, w_out, w_pre, w_post):
        m = x_in.shape[2]
        x = x_in[0]; dy = dy_out[0]; pos = positions[0]
        wq = w_query.reshape(m, H*D); wk = w_key.reshape(m, D); wv = w_value.reshape(m, D); wo = w_out.reshape(H*D, m)
        wpre = w_pre.reshape(1, m); wpost = w_post.reshape(1, m)
        idx = lax.axis_index("cp")

        def swap(v, mask):
            return lax.ppermute(v, "cp", [(i, i^mask) for i in range(4)])

        xs = swap(x[CH:], 1)
        ps = swap(pos[CH:], 1)
        dys = swap(dy[CH:], 1)
        xr0 = swap(x[:CH], 2)
        xr1 = swap(x[CH:], 3)
        pr0 = swap(pos[:CH], 2)
        pr1 = swap(pos[CH:], 3)
        dyr0 = swap(dy[:CH], 2)
        dyr1 = swap(dy[CH:], 3)
        xl = jnp.concatenate([x[:CH], xs])
        dyl = jnp.concatenate([dy[:CH], dys])
        xr = jnp.concatenate([xr0, xr1])
        dyr = jnp.concatenate([dyr0, dyr1])
        cl, sl = tables(jnp.concatenate([pos[:CH], ps]))
        cr, sr = tables(jnp.concatenate([pr0, pr1]))

        def ids_of(i):
            return [2*i, 2*(i^1)+1]
        own = ids_of(idx); sib = ids_of(idx^1); rem = ids_of(idx^2); rsib = ids_of(idx^3)
        upper = idx >= 2
        far = [jnp.where(upper, g, 99) for g in rem+rsib]
        ids_l = jnp.stack(own+own+sib+far).astype(jnp.int32)
        ids_r = jnp.stack(rem+own+sib+rem+rsib).astype(jnp.int32)

        al, ql, kl, vl = proj(xl, cl, sl, wpre, wq, wk, wv)
        kvl = jnp.stack([kl, vl])
        kvs = swap(kvl, 1)
        kvf = lax.ppermute(kvl, "cp", [(0,2),(1,3)])
        kvfs = swap(kvf, 1)
        def slots(*parts):
            s = jnp.concatenate([p.reshape(2, 2, CH, D) for p in parts], axis=1)
            return s[0], s[1]
        k8, v8 = slots(kvl, kvs, kvf, kvfs)
        ol, olb, l2l = flash_fwd(ids_l, ql, k8, v8)
        yl, dol, dwo, dwpost = post(olb, xl, dyl, wpost, wo, None)
        z8 = jnp.zeros((8, CH, D), jnp.float32)
        dql, dk8, dv8 = flash_bwd(ids_l, ql, dol, ol, l2l, k8, v8, cl, sl, z8, z8)

        ar, qr, kr, vr = proj(xr, cr, sr, wpre, wq, wk, wv)
        kvr = jnp.stack([kr, vr])
        kvrs = swap(kvr, 1)
        k8, v8 = slots(kvl, kvs, kvr, kvrs)
        orr, orb, l2r = flash_fwd(ids_r, qr, k8, v8)
        _, dor, dwo, _ = post(orb, xr, dyr, wpost, wo, dwo)
        dqr, dk8, dv8 = flash_bwd(ids_r, qr, dor, orr, l2r, k8, v8, cr, sr, dk8, dv8)

        def mine(g):
            return jnp.concatenate([g[0:2], g[4:6]]).reshape(2048, D)
        def theirs(g):
            return jnp.concatenate([g[2:4], g[6:8]]).reshape(2048, D)
        dkv_in = swap(jnp.stack([theirs(dk8), theirs(dv8)]), 1)
        dk = mine(dk8)+dkv_in[0]
        dv = (mine(dv8)+dkv_in[1]).astype(jnp.bfloat16)
        c = jnp.concatenate([cl, cr]); s = jnp.concatenate([sl, sr])
        f = dk[:, :128]; g = dk[:, 128:]
        dk = jnp.concatenate([f*c+g*s, g*c-f*s], axis=1).astype(jnp.bfloat16)
        dwq, dwk, dwv, dxl, dwpre = last(jnp.concatenate([al, ar]), jnp.concatenate([dql, dqr]), dk, dv, xl, dyl, wpre, wq, wk, wv)

        def unswap(v):
            return jnp.concatenate([v[:CH], swap(v[CH:], 1)])[None]
        def pair_sum(v):
            return v+swap(v, 1)
        def all_sum(v):
            v = pair_sum(v)
            return v+swap(v, 2)
        return (unswap(yl), unswap(dxl), pair_sum(dwq).reshape(m, H, D), pair_sum(dwk).reshape(m, 1, D), pair_sum(dwv).reshape(m, 1, D),
                pair_sum(dwo).reshape(H, D, m), all_sum(dwpre)[0], all_sum(dwpost)[0])

    seq = P("dp", "cp", None)
    in_specs = (seq, P("dp", "cp"), seq, P(), P(), P(), P(), P(), P())
    out_specs = (seq, seq, P("dp", None, None), P("dp", None, None), P("dp", None, None), P("dp", None, None), P("dp"), P("dp"))
    return jax.shard_map(local_step, mesh=mesh, in_specs=in_specs, out_specs=out_specs, check_vma=False)
```

time: 668 us -> 411 us (0.62)
  matrix products: 264 us -> 0 us
  Pallas kernels: 0 us -> 208 us
  waiting for transfers between devices: 212 us -> 89.2 us
  local copies, waits for them, and re-layouts: 73.1 us -> 48.6 us
  other arithmetic: 66.1 us -> 43.8 us
  between operations: 15 us -> 1.23 us
  blocking collectives: 11.9 us -> 0 us
    dot_general x39 -> x0, matrix products: 264 us -> none  [the longest x4 49.7 us: gradient_block(): jnp.einsum('bqngd,bknd->bnqgk', d_attn, value_blk, preferred_element_type...]
    pallas_call x0 -> x9, Pallas kernels: none -> 208 us  [the longest x2 90.9 us: flash_bwd(): pl.pallas_call(functools.partial(bwd_kernel, nslot=ns, sub=sub), grid_spe...]
    psum x1 -> x0, waiting for transfers between devices: 175 us -> none  [local_step(): lax.psum((dw_query_part, dw_key_part, dw_value_part, dw_out_part, dw_pre_...]
    ppermute x26 -> x24, waiting for transfers between devices: 37.1 us -> 89.2 us  [the longest x23 83.5 us: swap(): return lax.ppermute(v, 'cp', [(i, i ^ mask) for i in range(4)])]
    while x34 -> x0, local copies, waits for them, and re-layouts: 31.6 us -> none  [the longest x5 14.5 us: local_step(): lax.fori_loop(1, groups, backward_body, (dquery_sum, key_rot, value_proj,...]
    reduce_sum x7 -> x0, other arithmetic: 27.7 us -> none  [the longest x4 22.3 us: absorb(): run_sum = run_sum * rescale + jnp.sum(weights, axis=-1)]
    psum x1 -> x0, blocking collectives: 11.9 us -> none  [local_step(): lax.psum((dw_query_part, dw_key_part, dw_value_part, dw_out_part, dw_pre_...]
    concatenate x3 -> x11, other arithmetic: 6.1 us -> 17.2 us  [the longest x1 3.13 us: slots(): s = jnp.concatenate([p.reshape(2, 2, CH, D) for p in parts], axis=1)]
  transfers between devices with their start and end apart: 27 -> 24, of which waited for: 7 -> 7; matrix products, arithmetic and copies ran while one was open for 29% -> 15% of each run, Pallas kernels for 0% -> 10%
where the time goes in v1:
time: 411 us; the launch traced here: 407 us
  Pallas kernels  208 us (51%)
  waiting for transfers between devices  89.2 us (22%)
  local copies, waits for them, and re-layouts  48.6 us (12%)
  other arithmetic  43.8 us (11%)
  starting transfers between devices  16.3 us (4%)
    pallas_call x2, Pallas kernels, flash_bwd(): pl.pallas_call(functools.partial(bwd_kernel, nslot=ns, sub=sub), grid_spe...  90.9 us
    ppermute x23, waiting for transfers between devices, swap(): return lax.ppermute(v, 'cp', [(i, i ^ mask) for i in range(4)])  83.5 us
    pallas_call x2, Pallas kernels, flash_fwd(): pl.pallas_call(functools.partial(fwd_kernel, nslot=ns, sub=sub), grid_spe...  40.2 us
    pallas_call x2, Pallas kernels, post(): pl.pallas_call(functools.partial(post_kernel, first=first), grid=(t // BR...  37.1 us
    pallas_call x1, Pallas kernels, last(): pl.pallas_call(last_kernel, grid=(t // BR,), in_specs=[pl.BlockSpec((BR,...  22.9 us
    unnamed x52, local copies, waits for them, and re-layouts  21.1 us
    pallas_call x2, Pallas kernels, proj(): pl.pallas_call(proj_kernel, grid=(t // BR,), in_specs=[pl.BlockSpec((BR,...  17 us
    ppermute x23, starting transfers between devices, swap(): return lax.ppermute(v, 'cp', [(i, i ^ mask) for i in range(4)])  13.2 us
  transfers between devices with their start and end apart: 24, of which 7 were waited for; matrix products, arithmetic and copies ran while one was open for 15% of the time, Pallas kernels for 10%

profile of v1, /device:TPU:0, one launch (start us, length us, event | category | flops | bytes accessed | tf_op | source)
XLA Modules:
  0.0 407.3 jit_solution(13520609313688421835)
XLA Ops:
  0.6 0.7 fusion.7
  1.3 2.8 collective-permute-start.10
  4.1 0.7 collective-permute-start.1
  4.8 2.8 slice_bitcast_fusion.9
  7.8 2.0 collective-permute-start.9
  9.8 1.2 slice_bitcast_fusion.7
  11.0 2.0 copy.19
  12.9 0.6 reshape.118.wp_ref
  13.5 0.9 collective-permute-start.7
  14.5 22.1 %collective-permute-done.9 = s32[512]{0:T(512)S(1)} collective-permute-done((s32[512]{0:T(512)S(1)}, s32[512]{0:T(512)S(1)}, u32[]{:S(2)}, u32[]{:S(2)}) %collective-permute-start.9) | collective-permute-done | bytes 2080 | tf_op jit(solution)/shard_map/ppermute | solution.py:300
  36.6 5.4 %multiply_sine_fusion = (f32[1024,128]{1,0:T(8,128)}, f32[1024,128]{1,0:T(8,128)}, f32[1024,128]{1,0:T(8,128)}, f32[1024,128]{1,0:T(8,128)}) fusion(f32[1024]{0:T(1024)S(1)} %add_convert_fusion.2, f32[128]{0:T(128)S(1)} %multiply_power_fusion, f32[1024]{0:T(1024)S(1)} %add_convert_fusion.1), kind=kLoop, calls=%fused_computation.37 | loop fusion | flops 262144 | bytes 2105856 | tf_op jit(solution)/shard_map/sin | solution.py:289
  42.0 1.6 pad_maximum_fusion.6.x_ref
  43.6 8.5 %proj.2 = (bf16[1024,1152]{1,0:T(8,128)(2,1)}, bf16[1024,1024]{1,0:T(8,128)(2,1)}, bf16[1024,256]{1,0:T(8,128)(2,1)}, bf16[1024,256]{1,0:T(8,128)(2,1)}) custom-call(bf16[1024,1152]{1,0:T(8,128)(2,1)} %pad_maximum_fusion.6.x_ref, f32[1024,128]{1,0:T(8,128)} %get-tuple-element.110.cos_ref, f32[1024,128]{1,0:T(8,128)} %get-tuple-element.111.sin_ref, ...), custom_call_target="tpu_custom_call" | custom-call | flops 3623878656 | bytes 9437184 | tf_op jit(solution)/shard_map/proj/pallas_call | solution.py:190
  52.1 2.3 pad_maximum_fusion.13
  54.4 3.1 collective-permute-start.3
  57.5 4.4 %collective-permute-done.7 = bf16[512,1152]{1,0:T(8,128)(2,1)} collective-permute-done((bf16[512,1152]{1,0:T(8,128)(2,1)S(1)}, bf16[512,1152]{1,0:T(8,128)(2,1)}, u32[]{:S(2)}, u32[]{:S(2)}) %collective-permute-start.7) | collective-permute-done | bytes 1179680 | tf_op jit(solution)/shard_map/ppermute | solution.py:300
  61.9 1.4 constant_dynamic-update-slice_fusion.1
  63.5 1.4 copy-done.17
  64.9 8.5 %proj.3 = (bf16[1024,1152]{1,0:T(8,128)(2,1)}, bf16[1024,1024]{1,0:T(8,128)(2,1)}, bf16[1024,256]{1,0:T(8,128)(2,1)}, bf16[1024,256]{1,0:T(8,128)(2,1)}) custom-call(bf16[1024,1152]{1,0:T(8,128)(2,1)} %copy-done.17, f32[1024,128]{1,0:T(8,128)} %get-tuple-element.105.cos_ref, f32[1024,128]{1,0:T(8,128)} %get-tuple-element.104.sin_ref, ...), custom_call_target="tpu_custom_call" | custom-call | flops 3623878656 | bytes 9437184 | tf_op jit(solution)/shard_map/proj/pallas_call | solution.py:190
  73.5 2.3 pad_maximum_fusion.14
  76.2 5.7 %collective-permute-done.3 = bf16[2,1024,256]{2,1,0:T(8,128)(2,1)} collective-permute-done((bf16[2,1024,256]{2,1,0:T(8,128)(2,1)}, bf16[2,1024,256]{2,1,0:T(8,128)(2,1)}, u32[]{:S(2)}, u32[]{:S(2)}) %collective-permute-start.3) | collective-permute-done | bytes 1048608 | tf_op jit(solution)/shard_map/ppermute | solution.py:329
  81.9 0.6 reshape.125.wp_ref
  82.5 0.7 stack.91.ids
  83.2 0.6 stack.102.ids
  83.8 2.8 pad_maximum_fusion.7.dy_ref
  86.7 45.5 %collective-permute-done.12 = bf16[512,1152]{1,0:T(8,128)(2,1)S(1)} collective-permute-done((bf16[512,1152]{1,0:T(8,128)(2,1)S(1)}, bf16[512,1152]{1,0:T(8,128)(2,1)S(1)}, u32[]{:S(2)}, u32[]{:S(2)}) %collective-permute-start.12) | collective-permute-done | bytes 1179680 | tf_op jit(solution)/shard_map/ppermute | solution.py:300
  132.2 3.0 pad_maximum_fusion.8.dy_ref
  135.2 3.1 pad_maximum_fusion.3
  138.3 2.2 slice_bitcast_fusion.4
  140.5 2.2 slice_bitcast_fusion.2
  142.8 14.0 %flash_fwd.2 = (f32[1024,1024]{1,0:T(8,128)}, bf16[1024,1024]{1,0:T(8,128)(2,1)}, f32[2,8,512]{2,1,0:T(8,128)}) custom-call(s32[10]{0:T(128)} %stack.91.ids, bf16[1024,1024]{1,0:T(8,128)(2,1)} %get-tuple-element.39.q_ref, bf16[8,512,256]{2,1,0:T(8,128)(2,1)} %get-tuple-element.93.k_ref, bf16[8,512,256]{2,1,0:T(8,128)(2,1)} %get-tuple-element.92.v_ref), custom_call_target="tpu_custom_call" | custom-call | tf_op jit(solution)/shard_map/flash_fwd/pallas_call | solution.py:61
  156.8 26.2 %flash_fwd.3 = (f32[1024,1024]{1,0:T(8,128)}, bf16[1024,1024]{1,0:T(8,128)(2,1)}, f32[2,8,512]{2,1,0:T(8,128)}) custom-call(s32[10]{0:T(128)} %stack.102.ids, bf16[1024,1024]{1,0:T(8,128)(2,1)} %get-tuple-element.50.q_ref, bf16[8,512,256]{2,1,0:T(8,128)(2,1)} %get-tuple-element.91.k_ref, bf16[8,512,256]{2,1,0:T(8,128)(2,1)} %get-tuple-element.90.v_ref), custom_call_target="tpu_custom_call" | custom-call | tf_op jit(solution)/shard_map/flash_fwd/pallas_call | solution.py:61
  183.0 0.6 broadcast_in_dim.16.dwi_ref
  183.6 17.8 %post.2 = (bf16[1024,1152]{1,0:T(8,128)(2,1)}, bf16[1024,1024]{1,0:T(8,128)(2,1)}, f32[1024,1152]{1,0:T(8,128)}, f32[1,1152]{1,0:T(1,128)}) custom-call(bf16[1024,1024]{1,0:T(8,128)(2,1)} %get-tuple-element.42.o_ref, bf16[1024,1152]{1,0:T(8,128)(2,1)} %pad_maximum_fusion.6.x_ref, bf16[1024,1152]{1,0:T(8,128)(2,1)} %pad_maximum_fusion.7.dy_ref, ...), custom_call_target="tpu_custom_call" | custom-call | flops 7247757312 | bytes 9437184 | tf_op jit(solution)/shard_map/post/pallas_call | solution.py:229
  201.4 19.3 %post.3 = (bf16[1024,1152]{1,0:T(8,128)(2,1)}, bf16[1024,1024]{1,0:T(8,128)(2,1)}, f32[1024,1152]{1,0:T(8,128)}, f32[1,1152]{1,0:T(1,128)}) custom-call(bf16[1024,1024]{1,0:T(8,128)(2,1)} %get-tuple-element.53.o_ref, bf16[1024,1152]{1,0:T(8,128)(2,1)} %copy-done.17, bf16[1024,1152]{1,0:T(8,128)(2,1)} %pad_maximum_fusion.8.dy_ref, ...), custom_call_target="tpu_custom_call" | custom-call | flops 7247757312 | bytes 9437184 | tf_op jit(solution)/shard_map/post/pallas_call | solution.py:229
  220.7 2.4 broadcast_in_dim.18.dki_ref.dvi_ref
  223.1 32.1 %flash_bwd.2 = (bf16[1024,1024]{1,0:T(8,128)(2,1)}, f32[8,512,256]{2,1,0:T(8,128)}, f32[8,512,256]{2,1,0:T(8,128)}) custom-call(s32[10]{0:T(128)} %stack.91.ids, bf16[1024,1024]{1,0:T(8,128)(2,1)} %get-tuple-element.39.q_ref, bf16[1024,1024]{1,0:T(8,128)(2,1)} %get-tuple-element.46.do_ref, f32[1024,1024]{1,0:T(8,128)} %get-tuple-element.47.o_ref, ...), custom_call_target="tpu_custom_call" | custom-call | tf_op jit(solution)/shard_map/flash_bwd/pallas_call | solution.py:145
  255.2 58.8 %flash_bwd.3 = (bf16[1024,1024]{1,0:T(8,128)(2,1)}, f32[8,512,256]{2,1,0:T(8,128)}, f32[8,512,256]{2,1,0:T(8,128)}) custom-call(s32[10]{0:T(128)} %stack.102.ids, bf16[1024,1024]{1,0:T(8,128)(2,1)} %get-tuple-element.50.q_ref, bf16[1024,1024]{1,0:T(8,128)(2,1)} %get-tuple-element.55.do_ref, f32[1024,1024]{1,0:T(8,128)} %get-tuple-element.56.o_ref, ...), custom_call_target="tpu_custom_call" | custom-call | tf_op jit(solution)/shard_map/flash_bwd/pallas_call | solution.py:145
  314.0 3.9 fusion.3
  318.6 1.3 copy-done.7
  319.9 0.7 copy-done.8
  320.6 2.5 pad_maximum_fusion.a_ref
  323.5 1.4 copy-done.13
  324.9 0.6 copy-done.14
  325.5 2.5 pad_maximum_fusion.4.dq_ref
  328.1 1.6 fusion.1
  330.0 1.1 pad_maximum_fusion.17.dk_ref
  331.1 22.9 %last.1 = (f32[1152,1024]{1,0:T(8,128)}, f32[1152,256]{1,0:T(8,128)}, f32[1152,256]{1,0:T(8,128)}, bf16[1024,1152]{1,0:T(8,128)(2,1)}, f32[1,1152]{1,0:T(1,128)}) custom-call(bf16[2048,1152]{1,0:T(8,128)(2,1)} %pad_maximum_fusion.a_ref, bf16[2048,1024]{1,0:T(8,128)(2,1)} %pad_maximum_fusion.4.dq_ref, bf16[2048,256]{1,0:T(8,128)(2,1)} %pad_maximum_fusion.17.dk_ref, ...), custom_call_target="tpu_custom_call" | custom-call | flops 10871635968 | bytes 18874368 | tf_op jit(solution)/shard_map/last/pallas_call | solution.py:271
  354.5 1.9 fusion.6
  357.0 8.4 %collective-permute-done.22 = f32[1,1152]{1,0:T(1,128)S(1)} collective-permute-done((f32[1,1152]{1,0:T(1,128)S(1)}, f32[1,1152]{1,0:T(1,128)S(1)}, u32[]{:S(2)}, u32[]{:S(2)}) %collective-permute-start.22) | collective-permute-done | bytes 4640 | tf_op jit(solution)/shard_map/ppermute | solution.py:300
  365.4 2.4 collective-permute-start.23
  367.9 1.6 collective-permute-done.23
  369.4 0.6 add_reduce_fusion
  370.1 1.6 maximum_bitcast_fusion
  371.7 0.5 collective-permute-start.17
  372.2 2.0 collective-permute-start.21
  374.5 1.4 collective-permute-done.21
  375.9 0.6 add_reduce_fusion.1
  376.5 6.4 %add.55 = f32[1024,1152]{1,0:T(8,128)} add(f32[1024,1152]{1,0:T(8,128)} %get-tuple-element.67, f32[1024,1152]{1,0:T(8,128)} %collective-permute-done.19) | non-fusion elementwise | flops 1179648 | bytes 14155776 | tf_op jit(solution)/shard_map/add | solution.py:363
  383.1 6.0 %copy.18 = f32[1152,1,256]{2,1,0:T(1,128)} copy(f32[1152,1,256]{2,0,1:T(8,128)S(1)} %add_bitcast_fusion) | data formatting | bytes 2359296
  389.3 6.2 %copy.17 = f32[1152,1,256]{2,1,0:T(1,128)} copy(f32[1152,1,256]{2,0,1:T(8,128)S(1)} %add_bitcast_fusion.1) | data formatting | bytes 2359296
  395.5 1.6 maximum_bitcast_fusion.1
  397.1 3.2 add.52
  400.3 6.7 %reshape.130 = f32[1152,4,256]{2,1,0:T(4,128)} reshape(f32[1152,1024]{1,0:T(8,128)} %add.52) | data formatting | bytes 9437184 | tf_op jit(solution)/shard_map/reshape | solution.py:367
  (92 shorter events, 3.9 us)
Async XLA Ops:
  1.3 8.4 %copy-start.4 = (bf16[1,1024,1152]{2,1,0:T(8,128)(2,1)S(1)}, bf16[1,1024,1152]{2,1,0:T(8,128)(2,1)}, u32[]{:S(2)}) copy-start(bf16[1,1024,1152]{2,1,0:T(8,128)(2,1)} %param.11) | copy-start | bytes 7077892
  1.3 13.1 %collective-permute-start.10 = (s32[512]{0:T(512)S(1)}, s32[512]{0:T(512)S(1)}, u32[]{:S(2)}, u32[]{:S(2)}) collective-permute-start(s32[512]{0:T(512)S(1)} %bitcast.92), channel_id=1, source_target_pairs={{0,3},{1,2},{2,1},{3,0},{4,7},{5,6},{6,5},{7,4}} | collective-permute-start | bytes 6152 | tf_op jit(solution)/shard_map/ppermute | solution.py:300
  4.1 9.4 %collective-permute-start.1 = (s32[512]{0:T(512)S(1)}, s32[512]{0:T(512)S(1)}, u32[]{:S(2)}, u32[]{:S(2)}) collective-permute-start(s32[512]{0:T(512)S(1)} %bitcast.93), channel_id=1, source_target_pairs={{0,1},{1,0},{2,3},{3,2},{4,5},{5,4},{6,7},{7,6}} | collective-permute-start | bytes 6152 | tf_op jit(solution)/shard_map/ppermute | solution.py:300
  7.6 34.4 %collective-permute-start = (bf16[512,1152]{1,0:T(8,128)(2,1)}, bf16[512,1152]{1,0:T(8,128)(2,1)S(1)}, u32[]{:S(2)}, u32[]{:S(2)}) collective-permute-start(bf16[512,1152]{1,0:T(8,128)(2,1)} %get-tuple-element.101), channel_id=1, source_target_pairs={{0,1},{1,0},{2,3},{3,2},{4,5},{5,4},{6,7},{7,6}} | collective-permute-start | bytes 3538952 | tf_op jit(solution)/shard_map/ppermute | solution.py:300
  7.6 55.7 %collective-permute-start.8 = (bf16[512,1152]{1,0:T(8,128)(2,1)}, bf16[512,1152]{1,0:T(8,128)(2,1)S(1)}, u32[]{:S(2)}, u32[]{:S(2)}) collective-permute-start(bf16[512,1152]{1,0:T(8,128)(2,1)} %get-tuple-element.101), channel_id=1, source_target_pairs={{0,3},{1,2},{2,1},{3,0},{4,7},{5,6},{6,5},{7,4}} | collective-permute-start | bytes 3538952 | tf_op jit(solution)/shard_map/ppermute | solution.py:300
  7.8 3.2 copy-start.5
  7.8 28.8 %collective-permute-start.9 = (s32[512]{0:T(512)S(1)}, s32[512]{0:T(512)S(1)}, u32[]{:S(2)}, u32[]{:S(2)}) collective-permute-start(s32[512]{0:T(512)S(1)} %bitcast.90), channel_id=1, source_target_pairs={{0,2},{1,3},{2,0},{3,1},{4,6},{5,7},{6,4},{7,5}} | collective-permute-start | bytes 6152 | tf_op jit(solution)/shard_map/ppermute | solution.py:300
  11.0 2.0 copy-start.18
  13.5 48.3 %collective-permute-start.7 = (bf16[512,1152]{1,0:T(8,128)(2,1)S(1)}, bf16[512,1152]{1,0:T(8,128)(2,1)}, u32[]{:S(2)}, u32[]{:S(2)}) collective-permute-start(bf16[512,1152]{1,0:T(8,128)(2,1)S(1)} %get-tuple-element.100), channel_id=1, source_target_pairs={{0,2},{1,3},{2,0},{3,1},{4,6},{5,7},{6,4},{7,5}} | collective-permute-start | bytes 3538952 | tf_op jit(solution)/shard_map/ppermute | solution.py:300
  14.4 61.3 %collective-permute-start.5 = (bf16[512,1152]{1,0:T(8,128)(2,1)}, bf16[512,1152]{1,0:T(8,128)(2,1)}, u32[]{:S(2)}, u32[]{:S(2)}) collective-permute-start(bf16[512,1152]{1,0:T(8,128)(2,1)} %get-tuple-element.99), channel_id=1, source_target_pairs={{0,1},{1,0},{2,3},{3,2},{4,5},{5,4},{6,7},{7,6}} | collective-permute-start | bytes 3538952 | tf_op jit(solution)/shard_map/ppermute | solution.py:300
  54.4 27.5 %collective-permute-start.3 = (bf16[2,1024,256]{2,1,0:T(8,128)(2,1)}, bf16[2,1024,256]{2,1,0:T(8,128)(2,1)}, u32[]{:S(2)}, u32[]{:S(2)}) collective-permute-start(bf16[2,1024,256]{2,1,0:T(8,128)(2,1)} %pad_maximum_fusion.13), channel_id=1, source_target_pairs={{0,2},{1,3},{4,6},{5,7}} | collective-permute-start | bytes 3145736 | tf_op jit(solution)/shard_map/ppermute | solution.py:329
  57.5 74.7 %collective-permute-start.13 = (bf16[512,1152]{1,0:T(8,128)(2,1)}, bf16[512,1152]{1,0:T(8,128)(2,1)}, u32[]{:S(2)}, u32[]{:S(2)}) collective-permute-start(bf16[512,1152]{1,0:T(8,128)(2,1)} %get-tuple-element.99), channel_id=1, source_target_pairs={{0,3},{1,2},{2,1},{3,0},{4,7},{5,6},{6,5},{7,4}} | collective-permute-start | bytes 3538952 | tf_op jit(solution)/shard_map/ppermute | solution.py:300
  61.9 70.3 %collective-permute-start.12 = (bf16[512,1152]{1,0:T(8,128)(2,1)S(1)}, bf16[512,1152]{1,0:T(8,128)(2,1)S(1)}, u32[]{:S(2)}, u32[]{:S(2)}) collective-permute-start(bf16[512,1152]{1,0:T(8,128)(2,1)S(1)} %get-tuple-element.98), channel_id=1, source_target_pairs={{0,2},{1,3},{2,0},{3,1},{4,6},{5,7},{6,4},{7,5}} | collective-permute-start | bytes 3538952 | tf_op jit(solution)/shard_map/ppermute | solution.py:300
  63.3 71.8 %collective-permute-start.2 = (bf16[2,1024,256]{2,1,0:T(8,128)(2,1)}, bf16[2,1024,256]{2,1,0:T(8,128)(2,1)}, u32[]{:S(2)}, u32[]{:S(2)}) collective-permute-start(bf16[2,1024,256]{2,1,0:T(8,128)(2,1)} %pad_maximum_fusion.13), channel_id=1, source_target_pairs={{0,1},{1,0},{2,3},{3,2},{4,5},{5,4},{6,7},{7,6}} | collective-permute-start | bytes 3145736 | tf_op jit(solution)/shard_map/ppermute | solution.py:300
  63.5 1.4 copy-start.17
  64.9 17.0 %copy-start.19 = (f32[1152]{0:T(1024)S(1)}, f32[1152]{0:T(1024)}, u32[]{:S(2)}) copy-start(f32[1152]{0:T(1024)} %param.17) | copy-start | bytes 13828
  75.8 59.4 %collective-permute-start.11 = (bf16[2,1024,256]{2,1,0:T(8,128)(2,1)}, bf16[2,1024,256]{2,1,0:T(8,128)(2,1)S(1)}, u32[]{:S(2)}, u32[]{:S(2)}) collective-permute-start(bf16[2,1024,256]{2,1,0:T(8,128)(2,1)} %pad_maximum_fusion.14), channel_id=1, source_target_pairs={{0,1},{1,0},{2,3},{3,2},{4,5},{5,4},{6,7},{7,6}} | collective-permute-start | bytes 3145736 | tf_op jit(solution)/shard_map/ppermute | solution.py:300
  81.9 53.2 %collective-permute-start.4 = (bf16[2,1024,256]{2,1,0:T(8,128)(2,1)}, bf16[2,1024,256]{2,1,0:T(8,128)(2,1)}, u32[]{:S(2)}, u32[]{:S(2)}) collective-permute-start(bf16[2,1024,256]{2,1,0:T(8,128)(2,1)} %collective-permute-done.3), channel_id=1, source_target_pairs={{0,1},{1,0},{2,3},{3,2},{4,5},{5,4},{6,7},{7,6}} | collective-permute-start | bytes 3145736 | tf_op jit(solution)/shard_map/ppermute | solution.py:300
  86.6 48.5 %copy-start.9 = (bf16[1024,256]{1,0:T(8,128)(2,1)S(1)}, bf16[1024,256]{1,0:T(8,128)(2,1)}, u32[]{:S(2)}) copy-start(bf16[1024,256]{1,0:T(8,128)(2,1)} %get-tuple-element.40) | copy-start | bytes 1572868
  86.7 48.5 %copy-start.10 = (bf16[1024,256]{1,0:T(8,128)(2,1)S(1)}, bf16[1024,256]{1,0:T(8,128)(2,1)}, u32[]{:S(2)}) copy-start(bf16[1024,256]{1,0:T(8,128)(2,1)} %get-tuple-element.41) | copy-start | bytes 1572868
  86.7 48.5 %copy-start.11 = (bf16[1024,256]{1,0:T(8,128)(2,1)S(1)}, bf16[1024,256]{1,0:T(8,128)(2,1)}, u32[]{:S(2)}) copy-start(bf16[1024,256]{1,0:T(8,128)(2,1)} %get-tuple-element.51) | copy-start | bytes 1572868
  86.7 48.5 %copy-start.12 = (bf16[1024,256]{1,0:T(8,128)(2,1)S(1)}, bf16[1024,256]{1,0:T(8,128)(2,1)}, u32[]{:S(2)}) copy-start(bf16[1024,256]{1,0:T(8,128)(2,1)} %get-tuple-element.52) | copy-start | bytes 1572868
  318.2 1.7 copy-start.7
  318.2 2.4 copy-start.8
  318.5 9.5 %collective-permute-start.14 = (f32[2,2048,256]{2,1,0:T(8,128)S(1)}, f32[2,2048,256]{2,1,0:T(8,128)S(1)}, u32[]{:S(2)}, u32[]{:S(2)}) collective-permute-start(f32[2,2048,256]{2,1,0:T(8,128)S(1)} %pad_maximum_fusion.5), channel_id=1, source_target_pairs={{0,1},{1,0},{2,3},{3,2},{4,5},{5,4},{6,7},{7,6}} | collective-permute-start | bytes 12582920 | tf_op jit(solution)/shard_map/ppermute | solution.py:300
  323.2 53.4 %collective-permute-start.19 = (f32[1024,1152]{1,0:T(8,128)}, f32[1024,1152]{1,0:T(8,128)}, u32[]{:S(2)}, u32[]{:S(2)}) collective-permute-start(f32[1024,1152]{1,0:T(8,128)} %get-tuple-element.67), channel_id=1, source_target_pairs={{0,1},{1,0},{2,3},{3,2},{4,5},{5,4},{6,7},{7,6}} | collective-permute-start | bytes 14155784 | tf_op jit(solution)/shard_map/ppermute | solution.py:300
  323.3 1.6 copy-start.13
  323.3 2.2 copy-start.14
  328.0 1.6 copy-start
  328.0 1.6 copy-start.1
  328.0 1.6 copy-start.2
  328.0 1.6 copy-start.3
  354.0 43.1 %collective-permute-start.16 = (f32[1152,1024]{1,0:T(8,128)}, f32[1152,1024]{1,0:T(8,128)S(1)}, u32[]{:S(2)}, u32[]{:S(2)}) collective-permute-start(f32[1152,1024]{1,0:T(8,128)} %get-tuple-element.64), channel_id=1, source_target_pairs={{0,1},{1,0},{2,3},{3,2},{4,5},{5,4},{6,7},{7,6}} | collective-permute-start | bytes 14155784 | tf_op jit(solution)/shard_map/ppermute | solution.py:300
  354.5 2.0 copy-start.16
  354.5 2.4 copy-start.20
  354.5 15.5 %copy-start.21 = (f32[1,1152]{1,0:T(1,128)S(1)}, f32[1,1152]{1,0:T(1,128)}, u32[]{:S(2)}) copy-start(f32[1,1152]{1,0:T(1,128)} %get-tuple-element.68) | copy-start | bytes 13828
  356.4 13.6 %collective-permute-start.6 = (bf16[512,1152]{1,0:T(8,128)(2,1)S(1)}, bf16[512,1152]{1,0:T(8,128)(2,1)S(1)}, u32[]{:S(2)}, u32[]{:S(2)}) collective-permute-start(bf16[512,1152]{1,0:T(8,128)(2,1)S(1)} %get-tuple-element.97), channel_id=1, source_target_pairs={{0,1},{1,0},{2,3},{3,2},{4,5},{5,4},{6,7},{7,6}} | collective-permute-start | bytes 3538952 | tf_op jit(solution)/shard_map/ppermute | solution.py:300
  356.5 26.5 %collective-permute-start.18 = (f32[1152,256]{1,0:T(8,128)S(1)}, f32[1152,256]{1,0:T(8,128)S(1)}, u32[]{:S(2)}, u32[]{:S(2)}) collective-permute-start(f32[1152,256]{1,0:T(8,128)S(1)} %copy-done.16), channel_id=1, source_target_pairs={{0,1},{1,0},{2,3},{3,2},{4,5},{5,4},{6,7},{7,6}} | collective-permute-start | bytes 3538952 | tf_op jit(solution)/shard_map/ppermute | solution.py:300
  357.0 8.5 %collective-permute-start.22 = (f32[1,1152]{1,0:T(1,128)S(1)}, f32[1,1152]{1,0:T(1,128)S(1)}, u32[]{:S(2)}, u32[]{:S(2)}) collective-permute-start(f32[1,1152]{1,0:T(1,128)S(1)} %copy-done.20), channel_id=1, source_target_pairs={{0,1},{1,0},{2,3},{3,2},{4,5},{5,4},{6,7},{7,6}} | collective-permute-start | bytes 13832 | tf_op jit(solution)/shard_map/ppermute | solution.py:300
  365.4 4.0 collective-permute-start.23
  370.1 2.2 collective-permute-start.20
  370.1 1.6 copy-start.15
  370.1 4.2 %copy-start.6 = (bf16[1024,1152]{1,0:T(8,128)(2,1)S(1)}, bf16[1024,1152]{1,0:T(8,128)(2,1)}, u32[]{:S(2)}) copy-start(bf16[1024,1152]{1,0:T(8,128)(2,1)} %get-tuple-element.63) | copy-start | bytes 7077892
  371.7 17.4 %collective-permute-start.17 = (f32[1152,256]{1,0:T(8,128)S(1)}, f32[1152,256]{1,0:T(8,128)S(1)}, u32[]{:S(2)}, u32[]{:S(2)}) collective-permute-start(f32[1152,256]{1,0:T(8,128)S(1)} %copy-done.15), channel_id=1, source_target_pairs={{0,1},{1,0},{2,3},{3,2},{4,5},{5,4},{6,7},{7,6}} | collective-permute-start | bytes 3538952 | tf_op jit(solution)/shard_map/ppermute | solution.py:300
  372.2 3.6 collective-permute-start.21
  375.9 19.6 %collective-permute-start.15 = (bf16[512,1152]{1,0:T(8,128)(2,1)S(1)}, bf16[512,1152]{1,0:T(8,128)(2,1)S(1)}, u32[]{:S(2)}, u32[]{:S(2)}) collective-permute-start(bf16[512,1152]{1,0:T(8,128)(2,1)S(1)} %get-tuple-element.95), channel_id=1, source_target_pairs={{0,1},{1,0},{2,3},{3,2},{4,5},{5,4},{6,7},{7,6}} | collective-permute-start | bytes 3538952 | tf_op jit(solution)/shard_map/ppermute | solution.py:300
  382.9 14.1 %slice-start = ((s8[4718592]{0:T(1024)(128)(4,1)}), s8[4194304]{0:T(1024)(128)(4,1)S(1)}, s32[]{:S(2)}) async-start(s8[4718592]{0:T(1024)(128)(4,1)} %bitcast.74), calls=%async_computation | async-start | bytes 8388608
  389.1 8.0 %slice-start.1 = ((s8[4718592]{0:T(1024)(128)(4,1)}), s8[524288]{0:T(1024)(128)(4,1)S(1)}, s32[]{:S(2)}) async-start(s8[4718592]{0:T(1024)(128)(4,1)} %bitcast.74), calls=%async_computation.1 | async-start | bytes 1048576

commit v2 on v0

v2 whole, which is shorter than its diff:
```python
import functools
import jax
import jax.numpy as jnp
from jax import lax
from jax.experimental import pallas as pl
from jax.experimental.pallas import tpu as pltpu
from jax.sharding import PartitionSpec as P

CH = 512
H = 4
D = 256
T = 1024
NS = 8
EPS = 1e-6
ROPE_BASE = 10000.0
CAPL = 50.0*1.4426950408889634
NN = (((1,),(0,)),((),()))
NT = (((1,),(1,)),((),()))
TN = (((0,),(0,)),((),()))
F32 = jnp.float32
BF16 = jnp.bfloat16
BR = 512


def dot(a, b, dims=NN):
    return lax.dot_general(a, b, dims, preferred_element_type=F32)


def params(limit=60):
    return pltpu.CompilerParams(dimension_semantics=("arbitrary",), vmem_limit_bytes=limit << 20)


def cost(us):
    return pl.CostEstimate(flops=int(us*4e7), bytes_accessed=1 << 20, transcendentals=0)


def row(i, *_):
    return (i, 0)


def const(*_):
    return (0, 0)


def whole(arr):
    return pl.BlockSpec(arr.shape, const, pipeline_mode=pl.Buffered(1))


ANY = pl.BlockSpec(memory_space=pl.ANY)


def load_pieces(kv_refs, kbuf, vbuf, sems):
    copies = []
    for n, kv in enumerate(kv_refs):
        for w, buf in enumerate((kbuf, vbuf)):
            copies.append(pltpu.make_async_copy(kv.at[w], buf.at[pl.ds(n*T, T)], sems.at[2*n+w]))
    for cp in copies:
        cp.start()
    for cp in copies:
        cp.wait()


def visit(ids, r, tile):
    def body(j, c):
        g = ids[4+j]
        @pl.when(g < r)
        def _():
            tile(j, False)
        @pl.when(g == r)
        def _():
            tile(j, True)
        return c
    lax.fori_loop(0, NS, body, 0)


def fwd_kernel(ids, q_ref, kv0, kv1, kv2, kv3, o_ref, ob_ref, l2_ref, kbuf, vbuf, acc, lacc, sems, *, sub):
    i = pl.program_id(0)
    r = ids[i]
    @pl.when(i == 0)
    def _():
        load_pieces((kv0, kv1, kv2, kv3), kbuf, vbuf, sems)
    acc[...] = jnp.zeros_like(acc)
    lacc[...] = jnp.zeros_like(lacc)
    def tile(j, masked):
        at = pl.ds(pl.multiple_of(j*CH, CH), CH)
        k = kbuf[at]
        v = vbuf[at]
        for h in range(H):
            for u in range(CH//sub):
                rows = slice(u*sub, (u+1)*sub)
                s = dot(q_ref[rows, h*D:(h+1)*D], k, NT)
                e = jnp.exp2(jnp.tanh(s*(1/50.0))*CAPL)
                if masked:
                    ri = lax.broadcasted_iota(jnp.int32, (sub, CH), 0)+u*sub
                    ci = lax.broadcasted_iota(jnp.int32, (sub, CH), 1)
                    e = jnp.where(ci <= ri, e, 0.0)
                lacc[h, rows] += e[:, :128]+e[:, 128:256]+e[:, 256:384]+e[:, 384:]
                acc[h, rows] += dot(e.astype(BF16), v)
    visit(ids, r, tile)
    for h in range(H):
        la = lacc[h]
        o = acc[h]/jnp.sum(la, axis=1, keepdims=True)
        o_ref[:, h*D:(h+1)*D] = o
        ob_ref[:, h*D:(h+1)*D] = o.astype(BF16)
        l2_ref[0, h:h+1, :] = jnp.log2(jnp.sum(la.T, axis=0, keepdims=True))


def flash_fwd(ids, q, kvs, sub=512, us=20):
    return pl.pallas_call(
        functools.partial(fwd_kernel, sub=sub),
        grid_spec=pltpu.PrefetchScalarGridSpec(
            num_scalar_prefetch=1, grid=(2*T//CH,),
            in_specs=[pl.BlockSpec((CH, H*D), row)]+[ANY]*4,
            out_specs=[pl.BlockSpec((CH, H*D), row), pl.BlockSpec((CH, H*D), row), pl.BlockSpec((1, 8, CH), lambda i, ids: (i, 0, 0))],
            scratch_shapes=[pltpu.VMEM((NS*CH, D), BF16), pltpu.VMEM((NS*CH, D), BF16), pltpu.VMEM((H, CH, D), F32),
                            pltpu.VMEM((H, CH, 128), F32), pltpu.SemaphoreType.DMA((8,))]),
        out_shape=[jax.ShapeDtypeStruct((2*T, H*D), F32), jax.ShapeDtypeStruct((2*T, H*D), BF16), jax.ShapeDtypeStruct((4, 8, CH), F32)],
        compiler_params=params(), cost_estimate=cost(us), name="flash_fwd",
    )(ids, q, *kvs)


def bwd_kernel(ids, q_ref, do_ref, o_ref, l2_ref, cl_ref, sl_ref, cr_ref, sr_ref, kv0, kv1, kv2, kv3, dq_ref, own_out, sib_out,
               kbuf, vbuf, dka, dva, dqt, pt, dst, dlt, sems, *, sub):
    i = pl.program_id(0)
    r = ids[i]
    @pl.when(i == 0)
    def _():
        dka[...] = jnp.zeros_like(dka)
        dva[...] = jnp.zeros_like(dva)
        load_pieces((kv0, kv1, kv2, kv3), kbuf, vbuf, sems)
    dqt[...] = jnp.zeros_like(dqt)
    for h in range(H):
        w = do_ref[:, h*D:(h+1)*D].astype(F32)*o_ref[:, h*D:(h+1)*D]
        w = w[:, :128]+w[:, 128:]
        dlt[h:h+1, :] = jnp.sum(w.T, axis=0, keepdims=True)
    steps = [(h, u) for h in range(H) for u in range(CH//sub)]
    def tile(j, masked):
        at = pl.ds(pl.multiple_of(j*CH, CH), CH)
        k = kbuf[at]
        v = vbuf[at]
        kt = k.T
        def score(h, u):
            cols = slice(u*sub, (u+1)*sub)
            return dot(k, q_ref[cols, h*D:(h+1)*D], NT), dot(v, do_ref[cols, h*D:(h+1)*D], NT)
        def soft(sd, h, u):
            s, dp = sd
            cols = slice(u*sub, (u+1)*sub)
            t = jnp.tanh(s*(1/50.0))
            p = jnp.exp2(t*CAPL-l2_ref[0, h:h+1, cols])
            if masked:
                ki = lax.broadcasted_iota(jnp.int32, (CH, sub), 0)
                qi = lax.broadcasted_iota(jnp.int32, (CH, sub), 1)+u*sub
                p = jnp.where(ki <= qi, p, 0.0)
            ds = (p*(dp-dlt[h:h+1, cols])*(1.0-t*t)).astype(BF16)
            c0 = h*CH+u*sub
            pt[:, c0:c0+sub] = p.astype(BF16)
            dst[:, c0:c0+sub] = ds
            return ds
        def dqs(ds, h, u):
            c0 = h*CH+u*sub
            dqt[:, c0:c0+sub] += dot(kt, ds)
        n = len(steps)
        s = score(*steps[0])
        e = None
        for m in range(n):
            s2 = score(*steps[m+1]) if m+1 < n else None
            e2 = soft(s, *steps[m])
            if e is not None:
                dqs(e, *steps[m-1])
            s, e = s2, e2
        dqs(e, *steps[n-1])
        dva[at] += sum(dot(pt[:, h*CH:(h+1)*CH], do_ref[:, h*D:(h+1)*D]) for h in range(H))
        dka[at] += sum(dot(dst[:, h*CH:(h+1)*CH], q_ref[:, h*D:(h+1)*D]) for h in range(H))
    visit(ids, r, tile)
    left = i < T//CH
    c = jnp.where(left, cl_ref[...], cr_ref[...])
    s = jnp.where(left, sl_ref[...], sr_ref[...])
    for h in range(H):
        x = dqt[:, h*CH:(h+1)*CH].T
        a = x[:, :128]
        b = x[:, 128:]
        dq_ref[:, h*D:h*D+128] = ((a*c+b*s)*(1/12.0)).astype(BF16)
        dq_ref[:, h*D+128:(h+1)*D] = ((b*c-a*s)*(1/12.0)).astype(BF16)
    @pl.when(i == pl.num_programs(0)-1)
    def _():
        lo = pl.ds(0, 2*T)
        hi = pl.ds(2*T, 2*T)
        out = [(dka.at[hi], sib_out.at[0]), (dva.at[hi], sib_out.at[1]), (dka.at[lo], own_out.at[0]), (dva.at[lo], own_out.at[1])]
        copies = [pltpu.make_async_copy(a, b, sems.at[n]) for n, (a, b) in enumerate(out)]
        for cp in copies:
            cp.start()
        for cp in copies:
            cp.wait()


def flash_bwd(ids, q, do, o, l2, cl, sl, cr, sr, kvs, sub=256, us=80):
    n = T//CH
    big = pl.BlockSpec((CH, H*D), row)
    left = pl.BlockSpec((CH, 128), lambda i, ids: (jnp.minimum(i, n-1), 0))
    right = pl.BlockSpec((CH, 128), lambda i, ids: (jnp.maximum(i-n, 0), 0))
    return pl.pallas_call(
        functools.partial(bwd_kernel, sub=sub),
        grid_spec=pltpu.PrefetchScalarGridSpec(
            num_scalar_prefetch=1, grid=(2*n,),
            in_specs=[big, big, big, pl.BlockSpec((1, 8, CH), lambda i, ids: (i, 0, 0)), left, left, right, right]+[ANY]*4,
            out_specs=[big, ANY, ANY],
            scratch_shapes=[pltpu.VMEM((NS*CH, D), BF16), pltpu.VMEM((NS*CH, D), BF16), pltpu.VMEM((NS*CH, D), F32), pltpu.VMEM((NS*CH, D), F32),
                            pltpu.VMEM((D, H*CH), F32), pltpu.VMEM((CH, H*CH), BF16), pltpu.VMEM((CH, H*CH), BF16), pltpu.VMEM((8, CH), F32),
                            pltpu.SemaphoreType.DMA((8,))]),
        out_shape=[jax.ShapeDtypeStruct((2*T, H*D), BF16)]+[jax.ShapeDtypeStruct((2, 2*T, D), F32)]*2,
        compiler_params=params(63), cost_estimate=cost(us), name="flash_bwd",
    )(ids, q, do, o, l2, cl, sl, cr, sr, *kvs)


def proj_kernel(*refs):
    x_ref, cos_ref, sin_ref, wp_ref, wq_ref, wk_ref, wv_ref = refs[:7]
    a_ref, q_ref, kv_ref = refs[-3:]
    x = x_ref[...].astype(F32)
    rinv = lax.rsqrt(jnp.mean(x*x, axis=-1, keepdims=True)+EPS)
    a = (x*rinv*(1.0+wp_ref[...])).astype(BF16)
    a_ref[...] = a.T
    c = cos_ref[...]
    s = sin_ref[...]
    def rope(y, scale):
        y = y.astype(BF16).astype(F32)
        f = y[:, :128]
        g = y[:, 128:]
        return ((f*c-g*s)*scale).astype(BF16), ((g*c+f*s)*scale).astype(BF16)
    for h in range(H):
        f, g = rope(dot(a, wq_ref[:, h*D:(h+1)*D]), 1/12.0)
        q_ref[:, h*D:h*D+128] = f
        q_ref[:, h*D+128:(h+1)*D] = g
    f, g = rope(dot(a, wk_ref[...]), 1.0)
    kv_ref[0, :, :128] = f
    kv_ref[0, :, 128:] = g
    kv_ref[1] = dot(a, wv_ref[...]).astype(BF16)


def proj(x, cos, sin, wp, wq, wk, wv, prev=()):
    t, m = x.shape
    n = t//BR
    at = n if prev else 0
    return pl.pallas_call(
        proj_kernel, grid=(n,),
        in_specs=[pl.BlockSpec((BR, m), row), pl.BlockSpec((BR, 128), row), pl.BlockSpec((BR, 128), row), pl.BlockSpec((1, m), const),
                  whole(wq), whole(wk), whole(wv)]+[ANY]*len(prev),
        out_specs=[pl.BlockSpec((m, BR), lambda i: (0, i+at)), pl.BlockSpec((BR, H*D), lambda i: (i+at, 0)), pl.BlockSpec((2, BR, D), lambda i: (0, i, 0))],
        out_shape=[jax.ShapeDtypeStruct((m, 2*t), BF16), jax.ShapeDtypeStruct((2*t, H*D), BF16), jax.ShapeDtypeStruct((2, t, D), BF16)],
        input_output_aliases={7: 0, 8: 1} if prev else {},
        compiler_params=params(), cost_estimate=cost(8), name="proj",
    )(x, cos, sin, wp, wq, wk, wv, *prev)


def post_kernel(o_ref, wp_ref, wo_ref, dy_ref, *rest, first):
    if first:
        x_ref, y_ref, do_ref, dwo_ref, dwp_ref = rest
    else:
        dwi_ref, _, do_ref, dwo_ref = rest
    i = pl.program_id(0)
    @pl.when(i == 0)
    def _():
        if first:
            dwp_ref[...] = jnp.zeros_like(dwp_ref)
            dwo_ref[...] = jnp.zeros_like(dwo_ref)
        else:
            dwo_ref[...] = dwi_ref[...]
    o = o_ref[...]
    z = dot(o, wo_ref[...]).astype(BF16).astype(F32)
    rinv = lax.rsqrt(jnp.mean(z*z, axis=-1, keepdims=True)+EPS)
    zh = z*rinv
    gain = 1.0+wp_ref[...]
    dy = dy_ref[...].astype(F32)
    if first:
        y_ref[...] = (x_ref[...].astype(F32)+(zh*gain).astype(BF16).astype(F32)).astype(BF16)
        dwp_ref[...] += jnp.sum(dy*zh, axis=0, keepdims=True)
    g = dy*gain
    dz = (rinv*(g-zh*jnp.mean(g*zh, axis=-1, keepdims=True))).astype(BF16)
    do_ref[...] = dot(dz, wo_ref[...], NT).astype(BF16)
    dwo_ref[...] += dot(o, dz, TN)


def post(o, dy, wp, wo, x=None, prev=()):
    t, m = dy.shape
    n = t//BR
    first = x is not None
    at = 0 if first else n
    spec = pl.BlockSpec((BR, m), row)
    in_specs = [pl.BlockSpec((BR, H*D), lambda i: (i+at, 0)), pl.BlockSpec((1, m), const), whole(wo), spec]
    out_specs = [pl.BlockSpec((BR, H*D), lambda i: (i+at, 0)), pl.BlockSpec((H*D, m), const)]
    out_shape = [jax.ShapeDtypeStruct((2*t, H*D), BF16), jax.ShapeDtypeStruct((H*D, m), F32)]
    if first:
        args = (x,)
        in_specs += [spec]
        out_specs = [spec]+out_specs+[pl.BlockSpec((1, m), const)]
        out_shape = [jax.ShapeDtypeStruct((t, m), BF16)]+out_shape+[jax.ShapeDtypeStruct((1, m), F32)]
    else:
        do, dwo = prev
        args = (dwo, do)
        in_specs += [whole(dwo), ANY]
    return pl.pallas_call(
        functools.partial(post_kernel, first=first), grid=(n,), in_specs=in_specs, out_specs=out_specs,
        out_shape=out_shape, input_output_aliases={} if first else {5: 0},
        compiler_params=params(), cost_estimate=cost(15), name="post",
    )(o, wp, wo, dy, *args)


def dwq_kernel(a_ref, q_ref, out):
    out[...] = dot(a_ref[...], q_ref[...])


def dwq_part(at, dq):
    m, t = at.shape
    n = dq.shape[1]
    col = lambda i: (0, i)
    return pl.pallas_call(
        dwq_kernel, grid=(n//D,),
        in_specs=[whole(at), pl.BlockSpec((t, D), col)],
        out_specs=pl.BlockSpec((m, D), col),
        out_shape=jax.ShapeDtypeStruct((m, n), F32),
        compiler_params=params(), cost_estimate=cost(7), name="dwq",
    )(at, dq)


def rope_back(dk, c, s, scale):
    f = dk[:, :128]
    g = dk[:, 128:]
    return jnp.concatenate([(f*c+g*s)*scale, (g*c-f*s)*scale], axis=1).astype(BF16)


def dwkv_kernel(a_ref, own_ref, in_ref, cl_ref, sl_ref, cr_ref, sr_ref, dwkv_ref, dkv_ref):
    i = pl.program_id(0)
    dk = own_ref[0]+in_ref[0]
    dv = (own_ref[1]+in_ref[1]).astype(BF16)
    left = i < T//BR
    dk = rope_back(dk, jnp.where(left, cl_ref[...], cr_ref[...]), jnp.where(left, sl_ref[...], sr_ref[...]), 1.0)
    dkv = jnp.concatenate([dk, dv], axis=1)
    dkv_ref[...] = dkv
    @pl.when(i == 0)
    def _():
        dwkv_ref[...] = dot(a_ref[...], dkv)
    @pl.when(i > 0)
    def _():
        dwkv_ref[...] += dot(a_ref[...], dkv)


def dwkv_part(at, own, got, cl, sl, cr, sr):
    m = at.shape[0]
    n = T//BR
    left = pl.BlockSpec((BR, 128), lambda i: (jnp.minimum(i, n-1), 0))
    right = pl.BlockSpec((BR, 128), lambda i: (jnp.maximum(i-n, 0), 0))
    pair = pl.BlockSpec((2, BR, D), lambda i: (0, i, 0))
    return pl.pallas_call(
        dwkv_kernel, grid=(2*n,),
        in_specs=[pl.BlockSpec((m, BR), lambda i: (0, i)), pair, pair, left, left, right, right],
        out_specs=[pl.BlockSpec((m, 2*D), const), pl.BlockSpec((BR, 2*D), row)],
        out_shape=[jax.ShapeDtypeStruct((m, 2*D), F32), jax.ShapeDtypeStruct((2*T, 2*D), BF16)],
        compiler_params=params(), cost_estimate=cost(6), name="dwkv",
    )(at, own, got, cl, sl, cr, sr)


def dx_kernel(dq_ref, dkv_ref, x_ref, dy_ref, wp_ref, wq_ref, wk_ref, wv_ref, dx_ref, dwp_ref):
    i = pl.program_id(0)
    @pl.when(i == 0)
    def _():
        dwp_ref[...] = jnp.zeros_like(dwp_ref)
    da = dot(dq_ref[...], wq_ref[...], NT)+dot(dkv_ref[:, :D], wk_ref[...], NT)+dot(dkv_ref[:, D:], wv_ref[...], NT)
    x = x_ref[...].astype(F32)
    rinv = lax.rsqrt(jnp.mean(x*x, axis=-1, keepdims=True)+EPS)
    xh = x*rinv
    dwp_ref[...] += jnp.sum(da*xh, axis=0, keepdims=True)
    g = da*(1.0+wp_ref[...])
    dx_ref[...] = (dy_ref[...].astype(F32)+rinv*(g-xh*jnp.mean(g*xh, axis=-1, keepdims=True))).astype(BF16)


def dx_part(dq, dkv, x, dy, wp, wq, wk, wv, rows=256):
    t, m = x.shape
    spec = pl.BlockSpec((rows, m), row)
    return pl.pallas_call(
        dx_kernel, grid=(t//rows,),
        in_specs=[pl.BlockSpec((rows, H*D), row), pl.BlockSpec((rows, 2*D), row), spec, spec, pl.BlockSpec((1, m), const), whole(wq), whole(wk), whole(wv)],
        out_specs=[spec, pl.BlockSpec((1, m), const)],
        out_shape=[jax.ShapeDtypeStruct((t, m), BF16), jax.ShapeDtypeStruct((1, m), F32)],
        compiler_params=params(), cost_estimate=cost(8), name="dx",
    )(dq, dkv, x, dy, wp, wq, wk, wv)


def sum_kernel(q0, q1, kv0, kv1, q_ref, k_ref, v_ref):
    for h in range(H):
        at = slice(h*D, (h+1)*D)
        q_ref[:, h, :] = q0[:, at]+q1[:, at]
    k_ref[:, 0, :] = kv0[:, :D]+kv1[:, :D]
    v_ref[:, 0, :] = kv0[:, D:]+kv1[:, D:]


def sum_parts(q0, q1, kv0, kv1, rows=144):
    m = q0.shape[0]
    out3 = lambda n: pl.BlockSpec((rows, n, D), lambda i: (i, 0, 0))
    return pl.pallas_call(
        sum_kernel, grid=(m//rows,),
        in_specs=[pl.BlockSpec((rows, H*D), row)]*2+[pl.BlockSpec((rows, 2*D), row)]*2,
        out_specs=[out3(H), out3(1), out3(1)],
        out_shape=[jax.ShapeDtypeStruct((m, n, D), F32) for n in (H, 1, 1)],
        compiler_params=params(), cost_estimate=cost(6), name="sums",
    )(q0, q1, kv0, kv1)


def tables(pos):
    inv = ROPE_BASE ** (jnp.arange(128, dtype=F32)*(-2.0/256))
    ang = pos.astype(F32)[:, None]*inv
    return jnp.cos(ang), jnp.sin(ang)


def solution(mesh):
    def local_step(x_in, positions, dy_out, w_query, w_key, w_value, w_out, w_pre, w_post):
        m = x_in.shape[2]
        x = x_in[0]
        dy = dy_out[0]
        wq = w_query.reshape(m, H*D)
        wk = w_key.reshape(m, D)
        wv = w_value.reshape(m, D)
        wo = w_out.reshape(H*D, m)
        wpre = w_pre.reshape(1, m)
        wpost = w_post.reshape(1, m)
        idx = lax.axis_index("cp")

        def swap(v, mask):
            return lax.ppermute(v, "cp", [(i, i ^ mask) for i in range(4)])

        order = (0, 3, 1, 2)
        ids = jnp.stack([2*(idx ^ g)+e for g in (0, 3)+order for e in range(2)]).astype(jnp.int32)

        def send(v):
            return swap(v, 3)

        pr = send(positions[0])
        xr = send(x)
        dyr = send(dy)
        cl, sl = tables(positions[0])
        at, q, kvl = proj(x, cl, sl, wpre, wq, wk, wv)
        kvs = swap(kvl, 1)
        pr = lax.optimization_barrier((pr, kvl))[0]
        cr, sr = tables(pr)
        at, q, kvr = proj(xr, cr, sr, wpre, wq, wk, wv, prev=(at, q))
        kvrs = swap(kvr, 1)
        kv4 = (kvl, kvr, kvs, kvrs)
        o, ob, l2 = flash_fwd(ids, q, kv4)
        y, do, dwo, dwpost = post(ob, dy, wpost, wo, x=x)
        do, dwo = post(ob, dyr, wpost, wo, prev=(do, dwo))
        dq, own, sib = flash_bwd(ids, q, do, o, l2, cl, sl, cr, sr, kv4)

        got = swap(sib, 1)
        dwq = dwq_part(at, dq)
        dwq_in = swap(dwq, 1)
        dwkv, dkv = dwkv_part(at, own, got, cl, sl, cr, sr)
        dwkv_in = swap(dwkv, 1)
        dx, dwpre = dx_part(dq, dkv, x, dy, wpre, wq, wk, wv)

        def all_sum(v):
            return (v+swap(v, 1))+(swap(v, 2)+swap(v, 3))

        dwo = dwo+swap(dwo, 1)
        dwq, dwk, dwv = sum_parts(dwq, dwq_in, dwkv, dwkv_in)
        return (y[None], dx[None], dwq, dwk, dwv, dwo.reshape(H, D, m), all_sum(dwpre)[0], all_sum(dwpost)[0])

    seq = P("dp", "cp", None)
    in_specs = (seq, P("dp", "cp"), seq, P(), P(), P(), P(), P(), P())
    out_specs = (seq, seq, P("dp", None, None), P("dp", None, None), P("dp", None, None), P("dp", None, None), P("dp"), P("dp"))
    return jax.shard_map(local_step, mesh=mesh, in_specs=in_specs, out_specs=out_specs, check_vma=False)
```

time: 668 us -> 330 us (0.49)
  matrix products: 264 us -> 0 us
  Pallas kernels: 0 us -> 206 us
  waiting for transfers between devices: 212 us -> 85.8 us
  local copies, waits for them, and re-layouts: 73.1 us -> 10 us
  other arithmetic: 66.1 us -> 15.2 us
  between operations: 15 us -> 0.71 us
  blocking collectives: 11.9 us -> 0 us
  starting transfers between devices: 18.3 us -> 11.4 us
    dot_general x39 -> x0, matrix products: 264 us -> none  [the longest x4 49.7 us: gradient_block(): jnp.einsum('bqngd,bknd->bnqgk', d_attn, value_blk, preferred_element_type...]
    pallas_call x0 -> x10, Pallas kernels: none -> 206 us  [the longest x1 78.4 us: flash_bwd(): pl.pallas_call(functools.partial(bwd_kernel, sub=sub), grid_spec=pltpu.Pr...]
    psum x1 -> x0, waiting for transfers between devices: 175 us -> none  [local_step(): lax.psum((dw_query_part, dw_key_part, dw_value_part, dw_out_part, dw_pre_...]
    ppermute x26 -> x15, waiting for transfers between devices: 37.1 us -> 85.8 us  [swap(): return lax.ppermute(v, 'cp', [(i, i ^ mask) for i in range(4)])]
    while x34 -> x0, local copies, waits for them, and re-layouts: 31.6 us -> none  [the longest x5 14.5 us: local_step(): lax.fori_loop(1, groups, backward_body, (dquery_sum, key_rot, value_proj,...]
    reduce_sum x7 -> x0, other arithmetic: 27.7 us -> none  [the longest x4 22.3 us: absorb(): run_sum = run_sum * rescale + jnp.sum(weights, axis=-1)]
    unnamed x131 -> x13, local copies, waits for them, and re-layouts: 28.5 us -> 7.45 us
    convert_element_type x5 -> x2, other arithmetic: 12.6 us -> 0.72 us  [tables(): ang = pos.astype(F32)[:, None] * inv]
  transfers between devices with their start and end apart: 27 -> 15, of which waited for: 7 -> 5; matrix products, arithmetic and copies ran while one was open for 29% -> 7% of each run, Pallas kernels for 0% -> 30%
where the time goes in v2:
time: 330 us; the launch traced here: 329 us
  Pallas kernels  206 us (62%)
  waiting for transfers between devices  85.8 us (26%)
  other arithmetic  15.2 us (5%)
  starting transfers between devices  11.4 us (3%)
  local copies, waits for them, and re-layouts  10 us (3%)
    ppermute x15, waiting for transfers between devices, swap(): return lax.ppermute(v, 'cp', [(i, i ^ mask) for i in range(4)])  85.8 us
    pallas_call x1, Pallas kernels, flash_bwd(): pl.pallas_call(functools.partial(bwd_kernel, sub=sub), grid_spec=pltpu.Pr...  78.4 us
    pallas_call x2, Pallas kernels, post(): pl.pallas_call(functools.partial(post_kernel, first=first), grid=(n,), in...  35.7 us
    pallas_call x1, Pallas kernels, flash_fwd(): pl.pallas_call(functools.partial(fwd_kernel, sub=sub), grid_spec=pltpu.Pr...  35 us
    pallas_call x2, Pallas kernels, proj(): pl.pallas_call(proj_kernel, grid=(n,), in_specs=[pl.BlockSpec((BR, m), ro...  18 us
    ppermute x15, starting transfers between devices, swap(): return lax.ppermute(v, 'cp', [(i, i ^ mask) for i in range(4)])  11.4 us
    pallas_call x1, Pallas kernels, dx_part(): pl.pallas_call(dx_kernel, grid=(t // rows,), in_specs=[pl.BlockSpec((rows...  10.2 us
    pallas_call x1, Pallas kernels, sum_parts(): pl.pallas_call(sum_kernel, grid=(m // rows,), in_specs=[pl.BlockSpec((row...  10 us
  transfers between devices with their start and end apart: 15, of which 5 were waited for; matrix products, arithmetic and copies ran while one was open for 7% of the time, Pallas kernels for 30%

profile of v2, /device:TPU:0, one launch (start us, length us, event | category | flops | bytes accessed | tf_op | source)
XLA Modules:
  0.0 329.2 jit_solution(9870251993839862603)
XLA Ops:
  0.6 2.8 collective-permute-start
  3.4 0.0 collective-permute-start.4
  3.4 1.7 collective-permute-start.1
  5.1 0.7 convert_element_type.10
  5.9 1.3 reshape.48.refs_3_.wp_ref
  7.2 3.7 %copy.20 = bf16[144,8,4,256]{3,1,2,0:T(8,128)(2,1)} copy(bf16[144,8,4,256]{3,2,1,0:T(4,128)(2,1)} %bitcast.38) | data formatting | bytes 4718592
  10.8 3.1 multiply_sine_fusion.1
  13.9 9.1 %proj.2 = (bf16[1152,2048]{1,0:T(8,128)(2,1)}, bf16[2048,1024]{1,0:T(8,128)(2,1)}, bf16[2,1024,256]{2,1,0:T(8,128)(2,1)}) custom-call(bf16[1024,1152]{1,0:T(8,128)(2,1)} %bitcast.23, f32[1024,128]{1,0:T(8,128)} %get-tuple-element.63.refs_1_.cl_ref, f32[1024,128]{1,0:T(8,128)} %get-tuple-element.62.refs_2_.sl_ref, f32[1,1152]{1,0:T(1,128)} %reshape.48.refs_3_.wp_ref, ...), custom_call_target="tpu_custom_call" | custom-call | flops 320000000 | bytes 1048576 | tf_op jit(solution)/shard_map/proj/pallas_call | solution.py:243
  23.0 0.7 collective-permute-start.2
  23.7 82.2 %collective-permute-done.1 = s32[1024]{0:T(1024)S(1)} collective-permute-done((s32[1024]{0:T(1024)}, s32[1024]{0:T(1024)S(1)}, u32[]{:S(2)}, u32[]{:S(2)}) %collective-permute-start.1) | collective-permute-done | bytes 4128 | tf_op jit(solution)/shard_map/ppermute | solution.py:427
  105.9 3.0 multiply_sine_fusion
  109.0 0.0 collective-permute-done.refs_0_
  109.0 0.0 copy-start.3
  109.0 1.4 copy-done.3
  110.4 0.0 copy-start.4
  110.4 8.9 %proj.3 = (bf16[1152,2048]{1,0:T(8,128)(2,1)}, bf16[2048,1024]{1,0:T(8,128)(2,1)}, bf16[2,1024,256]{2,1,0:T(8,128)(2,1)}) custom-call(bf16[1024,1152]{1,0:T(8,128)(2,1)} %copy-done.3, f32[1024,128]{1,0:T(8,128)} %get-tuple-element.61.refs_1_.cr_ref, f32[1024,128]{1,0:T(8,128)} %get-tuple-element.60.refs_2_.sr_ref, ...), custom_call_target="tpu_custom_call", output_to_operand_aliasing={{0}: (7, {}), {1}: (8, {})} | custom-call | flops 320000000 | bytes 1048576 | tf_op jit(solution)/shard_map/proj/pallas_call | solution.py:243
  119.2 0.1 collective-permute-start.3
  119.3 0.0 copy-done.4
  119.3 0.6 reshape.52.wp_ref
  119.9 0.7 stack.39.ids
  120.6 0.0 collective-permute-done.2.kv2
  120.6 0.0 copy-start
  120.6 1.5 collective-permute-done.3.kv3
  122.1 0.0 copy-start.1
  122.1 0.0 copy-done
  122.1 1.0 copy-done.1
  123.1 35.0 %flash_fwd.1 = (f32[2048,1024]{1,0:T(8,128)}, bf16[2048,1024]{1,0:T(8,128)(2,1)}, f32[4,8,512]{2,1,0:T(8,128)}) custom-call(s32[12]{0:T(128)} %stack.39.ids, bf16[2048,1024]{1,0:T(8,128)(2,1)} %get-tuple-element.38.q_ref, bf16[2,1024,256]{2,1,0:T(8,128)(2,1)} %get-tuple-element.34.kv0, bf16[2,1024,256]{2,1,0:T(8,128)(2,1)} %get-tuple-element.39.kv1, ...), custom_call_target="tpu_custom_call" | custom-call | flops 800000000 | bytes 1048576 | tf_op jit(solution)/shard_map/flash_fwd/pallas_call | solution.py:109
  158.1 18.2 %post.2 = (bf16[1024,1152]{1,0:T(8,128)(2,1)}, bf16[2048,1024]{1,0:T(8,128)(2,1)}, f32[1024,1152]{1,0:T(8,128)}, f32[1,1152]{1,0:T(1,128)}) custom-call(bf16[2048,1024]{1,0:T(8,128)(2,1)} %get-tuple-element.40.o_ref, f32[1,1152]{1,0:T(1,128)} %reshape.52.wp_ref, bf16[1024,1152]{1,0:T(8,128)(2,1)} %bitcast.29, bf16[1024,1152]{1,0:T(8,128)(2,1)} %bitcast.27, ...), custom_call_target="tpu_custom_call" | custom-call | flops 600000000 | bytes 1048576 | tf_op jit(solution)/shard_map/post/pallas_call | solution.py:300
  176.3 0.0 collective-permute-done.4.dy_ref
  176.3 17.4 %post.3 = (bf16[2048,1024]{1,0:T(8,128)(2,1)}, f32[1024,1152]{1,0:T(8,128)}) custom-call(bf16[2048,1024]{1,0:T(8,128)(2,1)} %get-tuple-element.40.o_ref, f32[1,1152]{1,0:T(1,128)} %reshape.52.wp_ref, bf16[1024,1152]{1,0:T(8,128)(2,1)} %bitcast.30, bf16[1024,1152]{1,0:T(8,128)(2,1)} %collective-permute-done.4.dy_ref, ...), custom_call_target="tpu_custom_call", output_to_operand_aliasing={{0}: (5, {})} | custom-call | flops 600000000 | bytes 1048576 | tf_op jit(solution)/shard_map/post/pallas_call | solution.py:300
  193.8 78.4 %flash_bwd.1 = (bf16[2048,1024]{1,0:T(8,128)(2,1)}, f32[2,2048,256]{2,1,0:T(8,128)}, f32[2,2048,256]{2,1,0:T(8,128)}) custom-call(s32[12]{0:T(128)} %stack.39.ids, bf16[2048,1024]{1,0:T(8,128)(2,1)} %get-tuple-element.38.q_ref, bf16[2048,1024]{1,0:T(8,128)(2,1)} %get-tuple-element.44.do_ref, f32[2048,1024]{1,0:T(8,128)} %get-tuple-element.45.o_ref, ...), custom_call_target="tpu_custom_call" | custom-call | flops 3200000000 | bytes 1048576 | tf_op jit(solution)/shard_map/flash_bwd/pallas_call | solution.py:201
  272.2 0.1 collective-permute-start.5
  272.4 0.4 collective-permute-start.8
  272.8 9.7 %dwq.1.q0 = f32[1152,1024]{1,0:T(8,128)} custom-call(bf16[1152,2048]{1,0:T(8,128)(2,1)} %get-tuple-element.48.a_ref, bf16[2048,1024]{1,0:T(8,128)(2,1)} %get-tuple-element.47.dq_ref.q_ref), custom_call_target="tpu_custom_call" | custom-call | flops 280000000 | bytes 1048576 | tf_op jit(solution)/shard_map/dwq/pallas_call | solution.py:315
  282.4 0.1 collective-permute-start.6
  282.6 0.0 collective-permute-done.5.in_ref
  282.6 0.0 copy-start.5
  282.6 9.2 %dwkv.1 = (f32[1152,512]{1,0:T(8,128)}, bf16[2048,512]{1,0:T(8,128)(2,1)}) custom-call(bf16[1152,2048]{1,0:T(8,128)(2,1)} %get-tuple-element.48.a_ref, f32[2,2048,256]{2,1,0:T(8,128)} %get-tuple-element.49.own_ref, f32[2,2048,256]{2,1,0:T(8,128)} %collective-permute-done.5.in_ref, f32[1024,128]{1,0:T(8,128)} %get-tuple-element.63.refs_1_.cl_ref, ...), custom_call_target="tpu_custom_call" | custom-call | flops 240000000 | bytes 1048576 | tf_op jit(solution)/shard_map/dwkv/pallas_call | solution.py:352
  291.8 0.4 collective-permute-start.7
  292.2 0.0 copy-done.5
  292.2 2.4 collective-permute-start.13
  294.6 0.0 collective-permute-start.14
  294.6 10.2 %dx.1 = (bf16[1024,1152]{1,0:T(8,128)(2,1)}, f32[1,1152]{1,0:T(1,128)}) custom-call(bf16[2048,1024]{1,0:T(8,128)(2,1)} %get-tuple-element.47.dq_ref.q_ref, bf16[2048,512]{1,0:T(8,128)(2,1)} %get-tuple-element.51.dkv_ref, bf16[1024,1152]{1,0:T(8,128)(2,1)} %bitcast.25, bf16[1024,1152]{1,0:T(8,128)(2,1)} %bitcast.28, f32[1,1152]{1,0:T(1,128)} %reshape.48.refs_3_.wp_ref, ...), custom_call_target="tpu_custom_call" | custom-call | flops 320000000 | bytes 1048576 | tf_op jit(solution)/shard_map/dx/pallas_call | solution.py:378
  304.8 0.0 collective-permute-done.13
  304.8 0.0 collective-permute-start.12
  304.8 0.0 collective-permute-done.14
  304.8 1.8 collective-permute-start.10
  306.7 0.0 collective-permute-done.12
  306.7 0.8 collective-permute-start.11
  307.5 1.2 collective-permute-done.10
  308.7 0.0 collective-permute-start.9
  308.7 0.6 add_reduce_fusion
  309.3 0.6 collective-permute-done.11
  309.9 0.1 collective-permute-done.9
  310.1 1.3 add_reduce_fusion.1
  311.4 0.0 collective-permute-done.8
  311.4 6.4 %add.39 = f32[1024,1152]{1,0:T(8,128)} add(f32[1024,1152]{1,0:T(8,128)} %get-tuple-element.57, f32[1024,1152]{1,0:T(8,128)} %collective-permute-done.8) | non-fusion elementwise | flops 1179648 | bytes 14155776 | tf_op jit(solution)/shard_map/add | solution.py:461
  317.8 0.0 collective-permute-done.6.q1
  317.8 0.0 collective-permute-done.7.kv1
  317.8 0.0 copy-start.2
  317.8 1.4 copy-done.2
  319.2 10.0 %sums.1 = (f32[1152,4,256]{2,1,0:T(4,128)}, f32[1152,1,256]{2,1,0:T(1,128)}, f32[1152,1,256]{2,1,0:T(1,128)}) custom-call(f32[1152,1024]{1,0:T(8,128)} %dwq.1.q0, f32[1152,1024]{1,0:T(8,128)} %collective-permute-done.6.q1, f32[1152,512]{1,0:T(8,128)} %get-tuple-element.53.kv0, f32[1152,512]{1,0:T(8,128)} %copy-done.2), custom_call_target="tpu_custom_call" | custom-call | flops 240000000 | bytes 1048576 | tf_op jit(solution)/shard_map/sums/pallas_call | solution.py:398
  (2 shorter events, 0.0 us)
Async XLA Ops:
  0.6 108.3 %collective-permute-start = (bf16[1024,1152]{1,0:T(8,128)(2,1)}, bf16[1024,1152]{1,0:T(8,128)(2,1)S(1)}, u32[]{:S(2)}, u32[]{:S(2)}) collective-permute-start(bf16[1024,1152]{1,0:T(8,128)(2,1)} %bitcast.22), channel_id=1, source_target_pairs={{0,3},{1,2},{2,1},{3,0},{4,7},{5,6},{6,5},{7,4}} | collective-permute-start | bytes 7077896 | tf_op jit(solution)/shard_map/ppermute | solution.py:427
  3.4 172.9 %collective-permute-start.4 = (bf16[1024,1152]{1,0:T(8,128)(2,1)}, bf16[1024,1152]{1,0:T(8,128)(2,1)}, u32[]{:S(2)}, u32[]{:S(2)}) collective-permute-start(bf16[1024,1152]{1,0:T(8,128)(2,1)} %bitcast.26), channel_id=1, source_target_pairs={{0,3},{1,2},{2,1},{3,0},{4,7},{5,6},{6,5},{7,4}} | collective-permute-start | bytes 7077896 | tf_op jit(solution)/shard_map/ppermute | solution.py:427
  3.4 102.5 %collective-permute-start.1 = (s32[1024]{0:T(1024)}, s32[1024]{0:T(1024)S(1)}, u32[]{:S(2)}, u32[]{:S(2)}) collective-permute-start(s32[1024]{0:T(1024)} %bitcast.39), channel_id=1, source_target_pairs={{0,3},{1,2},{2,1},{3,0},{4,7},{5,6},{6,5},{7,4}} | collective-permute-start | bytes 12296 | tf_op jit(solution)/shard_map/ppermute | solution.py:427
  23.0 97.6 %collective-permute-start.2 = (bf16[2,1024,256]{2,1,0:T(8,128)(2,1)}, bf16[2,1024,256]{2,1,0:T(8,128)(2,1)S(1)}, u32[]{:S(2)}, u32[]{:S(2)}) collective-permute-start(bf16[2,1024,256]{2,1,0:T(8,128)(2,1)} %get-tuple-element.34.kv0), channel_id=1, source_target_pairs={{0,1},{1,0},{2,3},{3,2},{4,5},{5,4},{6,7},{7,6}} | collective-permute-start | bytes 3145736 | tf_op jit(solution)/shard_map/ppermute | solution.py:427
  109.0 1.4 copy-start.3
  110.4 8.9 %copy-start.4 = (f32[1152]{0:T(1024)S(1)}, f32[1152]{0:T(1024)}, u32[]{:S(2)}) copy-start(f32[1152]{0:T(1024)} %param.17) | copy-start | bytes 13828
  119.2 2.9 collective-permute-start.3
  120.6 1.5 copy-start
  122.1 1.0 copy-start.1
  272.2 10.3 %collective-permute-start.5 = (f32[2,2048,256]{2,1,0:T(8,128)}, f32[2,2048,256]{2,1,0:T(8,128)}, u32[]{:S(2)}, u32[]{:S(2)}) collective-permute-start(f32[2,2048,256]{2,1,0:T(8,128)} %get-tuple-element.50), channel_id=1, source_target_pairs={{0,1},{1,0},{2,3},{3,2},{4,5},{5,4},{6,7},{7,6}} | collective-permute-start | bytes 12582920 | tf_op jit(solution)/shard_map/ppermute | solution.py:427
  272.4 39.0 %collective-permute-start.8 = (f32[1024,1152]{1,0:T(8,128)}, f32[1024,1152]{1,0:T(8,128)}, u32[]{:S(2)}, u32[]{:S(2)}) collective-permute-start(f32[1024,1152]{1,0:T(8,128)} %get-tuple-element.57), channel_id=1, source_target_pairs={{0,1},{1,0},{2,3},{3,2},{4,5},{5,4},{6,7},{7,6}} | collective-permute-start | bytes 14155784 | tf_op jit(solution)/shard_map/ppermute | solution.py:427
  282.4 35.4 %collective-permute-start.6 = (f32[1152,1024]{1,0:T(8,128)}, f32[1152,1024]{1,0:T(8,128)}, u32[]{:S(2)}, u32[]{:S(2)}) collective-permute-start(f32[1152,1024]{1,0:T(8,128)} %dwq.1.q0), channel_id=1, source_target_pairs={{0,1},{1,0},{2,3},{3,2},{4,5},{5,4},{6,7},{7,6}} | collective-permute-start | bytes 14155784 | tf_op jit(solution)/shard_map/ppermute | solution.py:427
  282.6 9.6 %copy-start.5 = (f32[1,1152]{1,0:T(1,128)S(1)}, f32[1,1152]{1,0:T(1,128)}, u32[]{:S(2)}) copy-start(f32[1,1152]{1,0:T(1,128)} %get-tuple-element.59) | copy-start | bytes 13828
  291.8 26.0 %collective-permute-start.7 = (f32[1152,512]{1,0:T(8,128)}, f32[1152,512]{1,0:T(8,128)S(1)}, u32[]{:S(2)}, u32[]{:S(2)}) collective-permute-start(f32[1152,512]{1,0:T(8,128)} %get-tuple-element.53.kv0), channel_id=1, source_target_pairs={{0,1},{1,0},{2,3},{3,2},{4,5},{5,4},{6,7},{7,6}} | collective-permute-start | bytes 7077896 | tf_op jit(solution)/shard_map/ppermute | solution.py:427
  292.2 12.6 %collective-permute-start.13 = (f32[1,1152]{1,0:T(1,128)S(1)}, f32[1,1152]{1,0:T(1,128)S(1)}, u32[]{:S(2)}, u32[]{:S(2)}) collective-permute-start(f32[1,1152]{1,0:T(1,128)S(1)} %copy-done.5), channel_id=1, source_target_pairs={{0,2},{1,3},{2,0},{3,1},{4,6},{5,7},{6,4},{7,5}} | collective-permute-start | bytes 13832 | tf_op jit(solution)/shard_map/ppermute | solution.py:427
  294.6 10.2 %collective-permute-start.14 = (f32[1,1152]{1,0:T(1,128)S(1)}, f32[1,1152]{1,0:T(1,128)S(1)}, u32[]{:S(2)}, u32[]{:S(2)}) collective-permute-start(f32[1,1152]{1,0:T(1,128)S(1)} %copy-done.5), channel_id=1, source_target_pairs={{0,3},{1,2},{2,1},{3,0},{4,7},{5,6},{6,5},{7,4}} | collective-permute-start | bytes 13832 | tf_op jit(solution)/shard_map/ppermute | solution.py:427
  304.8 1.9 collective-permute-start.12
  304.8 3.8 %collective-permute-start.10 = (f32[1,1152]{1,0:T(1,128)}, f32[1,1152]{1,0:T(1,128)S(1)}, u32[]{:S(2)}, u32[]{:S(2)}) collective-permute-start(f32[1,1152]{1,0:T(1,128)} %get-tuple-element.58), channel_id=1, source_target_pairs={{0,2},{1,3},{2,0},{3,1},{4,6},{5,7},{6,4},{7,5}} | collective-permute-start | bytes 13832 | tf_op jit(solution)/shard_map/ppermute | solution.py:427
  306.7 3.2 collective-permute-start.11
  308.7 1.4 collective-permute-start.9
  317.8 1.4 copy-start.2
